TPU v7x, 256 devices: a whole 4x4x8 slice. The times are simulated.
256 devices in a mesh: rows: 32 (over x, z_lo, core), cols: 8 (over y, z_hi).
Axes of the slice: x: 4, y: 4, z: 8 (z_hi: 2, z_lo: 4; z = z_hi * 4 + z_lo), core: 2. Of those that a mesh axis runs over, the one named last changes fastest.
Arguments:
- image: float32 [2048, 16384], P('rows', 'cols'), may hold values from -6 to 6
- cloud_mask: int32 [2048, 16384], P('rows', 'cols'), may hold values 0 or 1
- tile_weight: int32 [256, 128], P('rows', 'cols'), may hold values from 1 to 8
- owner: int32 [256], replicated, may hold values from 0 to 31, as said below
Outputs:
- solution: float32 [2048, 16384], P('rows', 'cols')
- objective: float32 [3], replicated
Inputs may be any that keep to these rules, and one draw needn't show every extreme that they name: `owner`: every index of rows owns exactly 8 blocks, and the 8 blocks b*8 to b*8 + 7 have 8 different owners for every b.
All inputs are finite; a program needn't handle non-finite values. No bound on the sum of `cloud_mask` on one device may be relied on, other than what follows from the above.
Results may differ from a plain program's by a relative error of at most 0.0001.
Values sent between devices are 32-bit elements; how exact they have to be, the bound alone decides.
A program may use at most 64 MiB of HBM per device.

v0:
```python
import jax
import jax.numpy as jnp
from jax import lax
from jax.sharding import Mesh
from jax.sharding import PartitionSpec as P

BR = 8
TW = 128
ITERS = 3
ROWS = ("rows_0", "rows_1", "rows_2")
COLS = ("cols_0", "cols_1")
ROWS_COLS = ("rows_0", "rows_1", "rows_2", "cols_0", "cols_1")


fidelity_scale = 0.25
tau_step = 0.35
sigma_step = 0.35
tv_weight = 0.3


def passed_along(block, axis, distance):
    devices = range(lax.axis_size(axis))
    route = [(i - distance, i) for i in devices if i - distance in devices]
    return lax.ppermute(block, axis, route)


def over_axes(array, axes):
    for axis in axes:
        array = lax.psum(array, axis)
    return array


def per_device(image, cloud_mask, tile_weight, owner):
    rows_here, width_here = image.shape
    blocks_here = rows_here // BR
    row_count = lax.axis_size(ROWS)
    col_count = lax.axis_size(COLS)
    own_row = lax.axis_index(ROWS)
    own_col = lax.axis_index(COLS)
    total_blocks = owner.shape[0]
    height_all = total_blocks * BR
    width_all = width_here * col_count
    pixel_total = height_all * width_all
    tile_count = width_here // TW
    clear_sky = (1 - cloud_mask).astype(jnp.float32).reshape(blocks_here, BR, tile_count, TW)
    fidelity = (
        fidelity_scale * tile_weight.astype(jnp.float32)[:, None, :, None] * clear_sky
    ).reshape(rows_here, width_here)
    local_index = jnp.arange(blocks_here, dtype=jnp.int32)
    home_blocks = own_row * blocks_here + local_index
    targets = owner[home_blocks]
    owned = jnp.argsort((owner != own_row).astype(jnp.int32), stable=True)[:blocks_here]
    senders = owned // blocks_here
    last_column = ((jnp.arange(width_here) == width_here - 1) & (own_col == col_count - 1))[None, :]
    has_next = (home_blocks + 1 < total_blocks)[:, None]
    has_prev = (home_blocks > 0)[:, None]
    primal = image
    extrap = image
    dual_rows = jnp.zeros_like(image)
    dual_cols = jnp.zeros_like(image)
    values = []
    for step in range(ITERS):
        shaped = extrap.reshape(blocks_here, BR, width_here)
        first_rows = shaped[:, 0, :]
        below_arriving = passed_along(first_rows[:1], ROWS, -1)
        follow = jnp.concatenate([first_rows[1:], below_arriving], axis=0)
        bottom = jnp.where(has_next, follow - shaped[:, -1, :], 0.0)
        grad_r = jnp.concatenate(
            [shaped[:, 1:, :] - shaped[:, :-1, :], bottom[:, None, :]], axis=1
        ).reshape(rows_here, width_here)
        right_edge = passed_along(extrap[:, 0][None, :], COLS, -1)
        grad_c = jnp.concatenate(
            [extrap[:, 1:] - extrap[:, :-1], right_edge[0][:, None] - extrap[:, -1:]], axis=1
        )
        grad_c = jnp.where(last_column, 0.0, grad_c)
        trial_rows = dual_rows + sigma_step * grad_r
        trial_cols = dual_cols + sigma_step * grad_c
        shrink = jnp.maximum(
            1.0, jnp.sqrt(trial_rows * trial_rows + trial_cols * trial_cols) / tv_weight
        )
        dual_rows = trial_rows / shrink
        dual_cols = trial_cols / shrink
        dual_shaped = dual_rows.reshape(blocks_here, BR, width_here)
        last_rows = dual_shaped[:, -1, :]
        arriving = passed_along(last_rows[-1:], ROWS, 1)
        leading = jnp.where(has_prev, jnp.concatenate([arriving, last_rows[:-1]], axis=0), 0.0)
        earlier_rows = jnp.concatenate([leading[:, None, :], dual_shaped[:, :-1, :]], axis=1)
        div_rows = (dual_shaped - earlier_rows).reshape(rows_here, width_here)
        left_edge = passed_along(dual_cols[:, -1][None, :], COLS, 1)
        div_cols = dual_cols - jnp.concatenate([left_edge[0][:, None], dual_cols[:, :-1]], axis=1)
        updated = (primal + tau_step * (div_rows + div_cols) + tau_step * fidelity * image) / (
            1.0 + tau_step * fidelity
        )
        misfit = updated - image
        partial_sum = jnp.sum(0.5 * fidelity * misfit * misfit) + tv_weight * jnp.sum(
            jnp.sqrt(grad_r * grad_r + grad_c * grad_c)
        )
        values.append(partial_sum)
        extrap = 2.0 * updated - primal
        primal = updated
    primal, values = (primal, values)
    empty = jnp.zeros((row_count, BR, width_here), jnp.float32)
    solution = lax.all_to_all(
        empty.at[targets].set(primal.reshape(blocks_here, BR, width_here)),
        ROWS,
        split_axis=0,
        concat_axis=0,
        tiled=True,
    )[senders].reshape(rows_here, width_here)
    objective = over_axes(jnp.stack(values), ROWS_COLS) / pixel_total
    return (solution, objective)


def solution(mesh):
    split = Mesh(
        mesh.devices.reshape(4, 4, 2, 4, 2), ("rows_0", "rows_1", "rows_2", "cols_0", "cols_1")
    )
    placed = (P(ROWS, COLS), P(ROWS, COLS), P(ROWS, COLS), P())
    return jax.shard_map(
        per_device, mesh=split, in_specs=placed, out_specs=(P(ROWS, COLS), P()), check_vma=False
    )
```

profile of v0, /device:TPU:70, one launch (start us, length us, event | category | flops | bytes accessed | tf_op | source)
XLA Modules:
  0.0 194.1 jit_solution(11662208459327383046)
XLA Ops:
  0.6 0.9 slice_bitcast_fusion.5
  1.6 1.9 collective-permute-start
  3.5 0.9 slice_reduce_fusion.5
  4.3 1.3 collective-permute-start.1
  5.6 1.3 slice_subtract_fusion.4
  7.4 0.9 broadcast_bitcast_fusion
  8.4 5.3 %collective-permute-done.1 = f32[1,64]{1,0:T(1,128)S(1)} collective-permute-done((f32[1,64]{1,0:T(1,128)S(1)}, f32[1,64]{1,0:T(1,128)S(1)}, u32[]{:S(2)}, u32[]{:S(2)}) %collective-permute-start.1) | collective-permute-done | bytes 288 | tf_op jit(solution)/shard_map/ppermute | solution.py:24
  14.5 2.1 %collective-permute-start.2 = (f32[1,2048]{1,0:T(1,128)S(1)}, f32[1,2048]{1,0:T(1,128)S(1)}, u32[]{:S(2)}, u32[]{:S(2)}) collective-permute-start(f32[1,2048]{1,0:T(1,128)S(1)} %slice_bitcast_fusion.4), channel_id=1, source_target_pairs={{0,8},{8,16},{16,24},{24,32},{32,40},{40,48},{48,56},{56,64},{64,7... | collective-permute-start | bytes 24584 | tf_op jit(solution)/shard_map/ppermute | solution.py:24
  17.1 8.6 %collective-permute-start.3 = (f32[1,64]{1,0:T(1,128)S(1)}, f32[1,64]{1,0:T(1,128)S(1)}, u32[]{:S(2)}, u32[]{:S(2)}) collective-permute-start(f32[1,64]{1,0:T(1,128)S(1)} %bitcast.185), channel_id=1, source_target_pairs={{0,1},{1,2},{2,3},{3,4},{4,5},{5,6},{6,7},{8,9},{9,10},{10,11},{11... | collective-permute-start | bytes 776 | tf_op jit(solution)/shard_map/ppermute | solution.py:24
  25.8 1.2 collective-permute-done.3
  27.3 3.2 %multiply_subtract_fusion.1 = (f32[64,2048]{1,0:T(8,128)S(1)}, f32[64,2048]{1,0:T(8,128)}, f32[64,2048]{1,0:T(8,128)}, f32[64,2048]{1,0:T(8,128)}) fusion(f32[64,2048]{1,0:T(8,128)S(1)} %copy-done.1, f32[64,2048]{1,0:T(8,128)S(1)} %fusion.35, f32[64,2047]{1,0:T(8,128)S(1)} %bitcast.155, f32[64,1]{1,0:T(8,128)S(1)} %copy.32, f32[8,7,2048]{2,1,0:T(8,128)S(1)} %bitcast.156, ...), kind=kLoop, calls=%fused_computation.74 | loop fusion | flops 3670016 | bytes 6293504 | tf_op jit(solution)/shard_map/sub | solution.py:99
  30.6 1.0 fusion.45
  31.6 1.0 slice_subtract_fusion.2
  32.6 1.3 collective-permute-start.5
  34.0 2.8 %collective-permute-start.4 = (f32[1,2048]{1,0:T(1,128)S(1)}, f32[1,2048]{1,0:T(1,128)S(1)}, u32[]{:S(2)}, u32[]{:S(2)}) collective-permute-start(f32[1,2048]{1,0:T(1,128)S(1)} %slice_bitcast_fusion.3), channel_id=1, source_target_pairs={{8,0},{16,8},{24,16},{32,24},{40,32},{48,40},{56,48},{64,56},{72,6... | collective-permute-start | bytes 24584 | tf_op jit(solution)/shard_map/ppermute | solution.py:24
  36.8 5.4 %collective-permute-done.5 = f32[1,64]{1,0:T(1,128)S(1)} collective-permute-done((f32[1,64]{1,0:T(1,128)S(1)}, f32[1,64]{1,0:T(1,128)S(1)}, u32[]{:S(2)}, u32[]{:S(2)}) %collective-permute-start.5) | collective-permute-done | bytes 288 | tf_op jit(solution)/shard_map/ppermute | solution.py:24
  42.6 2.9 %fusion.31 = (f32[8,8,2048]{2,1,0:T(8,128)S(1)}, f32[8,8,2048]{2,1,0:T(8,128)}) fusion(f32[8,8,2048]{2,1,0:T(8,128)S(1)} %fusion.34, f32[8,1,2048]{2,1,0:T(1,128)S(1)} %broadcast_select_fusion.4, f32[8,7,2048]{2,1,0:T(8,128)S(1)} %slice_subtract_fusion.3, f32[8,8,1]{2,1,0:T(8,128)S(1)} %bitcast.164, f32[8,8,2047]{2,1,0:T(8,128)} %fusion.45, ...), kind=kLoop, calls=%fused_computation.70 | loop fusion | flops 3145728 | bytes 3672064 | tf_op jit(solution)/shard_map/div | solution.py:81
  45.5 1.9 collective-permute-start.6
  48.1 8.7 %collective-permute-start.7 = (f32[1,64]{1,0:T(1,128)S(1)}, f32[1,64]{1,0:T(1,128)S(1)}, u32[]{:S(2)}, u32[]{:S(2)}) collective-permute-start(f32[1,64]{1,0:T(1,128)S(1)} %bitcast.182), channel_id=1, source_target_pairs={{0,1},{1,2},{2,3},{3,4},{4,5},{5,6},{6,7},{8,9},{9,10},{10,11},{11... | collective-permute-start | bytes 776 | tf_op jit(solution)/shard_map/ppermute | solution.py:24
  56.8 0.6 gather_fusion
  57.5 0.5 collective-permute-done.7
  58.3 3.5 %multiply_subtract_fusion = (f32[64,2048]{1,0:T(8,128)S(1)}, f32[64,2048]{1,0:T(8,128)}, f32[64,2048]{1,0:T(8,128)}) fusion(f32[64,2048]{1,0:T(8,128)} %get-tuple-element.17, f32[64,2048]{1,0:T(8,128)S(1)} %copy-done.1, f32[64,2048]{1,0:T(8,128)} %get-tuple-element.18, f32[64,2048]{1,0:T(8,128)S(1)} %fusion.32, f32[64,2047]{1,0:T(8,128)S(1)} %bitcast.154, ...), kind=kLoop, calls=%fused_computation.67 | loop fusion | flops 3538944 | bytes 6817792 | tf_op jit(solution)/shard_map/sub | solution.py:99
  61.9 1.0 fusion.44
  62.9 1.0 slice_subtract_fusion
  63.9 1.3 collective-permute-start.9
  65.3 2.8 %collective-permute-start.8 = (f32[1,2048]{1,0:T(1,128)S(1)}, f32[1,2048]{1,0:T(1,128)S(1)}, u32[]{:S(2)}, u32[]{:S(2)}) collective-permute-start(f32[1,2048]{1,0:T(1,128)S(1)} %slice_bitcast_fusion.1), channel_id=1, source_target_pairs={{8,0},{16,8},{24,16},{32,24},{40,32},{48,40},{56,48},{64,56},{72,6... | collective-permute-start | bytes 24584 | tf_op jit(solution)/shard_map/ppermute | solution.py:24
  68.1 5.4 %collective-permute-done.9 = f32[1,64]{1,0:T(1,128)S(1)} collective-permute-done((f32[1,64]{1,0:T(1,128)S(1)}, f32[1,64]{1,0:T(1,128)S(1)}, u32[]{:S(2)}, u32[]{:S(2)}) %collective-permute-start.9) | collective-permute-done | bytes 288 | tf_op jit(solution)/shard_map/ppermute | solution.py:24
  73.9 2.2 %maximum_divide_fusion = f32[8,8,2048]{2,1,0:T(8,128)S(1)} fusion(f32[8,8,2048]{2,1,0:T(8,128)} %get-tuple-element.15, f32[8,8,1]{2,1,0:T(8,128)S(1)} %bitcast.166, f32[8,8,2047]{2,1,0:T(8,128)} %fusion.44, f32[8,1,2048]{2,1,0:T(1,128)S(1)} %broadcast_select_fusion.3, f32[8,7,2048]{2,1,0:T(8,128)S(1)} %slice_subtract_fusion.1, ...), kind=kLoop, calls=%fused_computation.64 | loop fusion | flops 3014656 | bytes 3147776 | tf_op jit(solution)/shard_map/div | solution.py:81
  76.2 2.1 %collective-permute-start.10 = (f32[1,2048]{1,0:T(1,128)S(1)}, f32[1,2048]{1,0:T(1,128)S(1)}, u32[]{:S(2)}, u32[]{:S(2)}) collective-permute-start(f32[1,2048]{1,0:T(1,128)S(1)} %slice_bitcast_fusion), channel_id=1, source_target_pairs={{0,8},{8,16},{16,24},{24,32},{32,40},{40,48},{48,56},{56,64},{64,7... | collective-permute-start | bytes 24584 | tf_op jit(solution)/shard_map/ppermute | solution.py:24
  78.9 8.7 %collective-permute-start.11 = (f32[1,64]{1,0:T(1,128)S(1)}, f32[1,64]{1,0:T(1,128)S(1)}, u32[]{:S(2)}, u32[]{:S(2)}) collective-permute-start(f32[1,64]{1,0:T(1,128)S(1)} %bitcast.186), channel_id=1, source_target_pairs={{0,1},{1,2},{2,3},{3,4},{4,5},{5,6},{6,7},{8,9},{9,10},{10,11},{11... | collective-permute-start | bytes 776 | tf_op jit(solution)/shard_map/ppermute | solution.py:24
  87.6 0.5 fusion.38
  88.2 0.7 collective-permute-done.11
  88.9 0.5 copy-done.21
  89.3 0.7 copy.38
  90.0 0.8 broadcast_select_fusion
  90.8 4.3 %fusion = (f32[]{:T(128)}, f32[]{:T(128)}, f32[]{:T(128)}, f32[64,2048]{1,0:T(8,128)}) fusion(f32[64,2048]{1,0:T(8,128)S(1)} %copy-done.5, f32[64,2048]{1,0:T(8,128)S(1)} %copy-done.1, f32[64,2048]{1,0:T(8,128)} %get-tuple-element.18, f32[64,2048]{1,0:T(8,128)} %get-tuple-element.12, f32[64,2047]{1,0:T(8,128)} %bitcast.159, f32[64,1]{1,0:T(8,128)S(1)} %copy.38, ...), kind=kLoop, calls=%fused_computation.6 | loop fusion | flops 5111805 | bytes 5769228 | tf_op jit(solution)/shard_map/reduce_sum | solution.py:95
  95.1 1.5 broadcast_in_dim.76
  96.7 2.5 %scatter_fusion = f32[32,8,2048]{2,1,0:T(8,128)} fusion(f32[32,8,2048]{2,1,0:T(8,128)} %broadcast_in_dim.76, s32[8]{0:T(128)S(1)} %copy-done.20, f32[8,8,2048]{2,1,0:T(8,128)S(1)} %bitcast.160), kind=kCustom, calls=%fused_computation.2 | custom fusion | bytes 1572896 | tf_op jit(solution)/shard_map/scatter | solution.py:104
  99.2 10.0 %all-to-all-start = ((f32[32,8,2048]{2,1,0:T(8,128)}), f32[32,8,2048]{2,1,0:T(8,128)}, u32[]{:S(2)}, u32[]{:S(2)}) async-start(f32[32,8,2048]{2,1,0:T(8,128)} %scatter_fusion), calls=%async_computation | async-start | bytes 4194304 | tf_op jit(solution)/shard_map/all_to_all | solution.py:103
  109.2 1.5 sqrt_reduce_fusion.2
  114.6 9.5 %psum.35 = f32[3]{0:T(128)S(1)} all-reduce(f32[3]{0:T(128)S(1)} %pad_maximum_fusion.3), channel_id=1, replica_groups=mesh['rows_0'=4,'rows_1'=4,'rows_2'=2,'cols_0'=4,'cols_1'=2] {'rows_0'}, use_global_device_ids=true, to_apply=%region_8.9 | all-reduce | flops 3 | bytes 24 | tf_op jit(solution)/shard_map/psum | solution.py:29
  124.1 35.1 %psum.36 = f32[3]{0:T(128)S(1)} all-reduce(f32[3]{0:T(128)S(1)} %psum.35), channel_id=1, replica_groups=mesh['rows_0'=4,'rows_1'=4,'rows_2'=2,'cols_0'=4,'cols_1'=2] {'rows_1'}, use_global_device_ids=true, to_apply=%region_9.10 | all-reduce | flops 3 | bytes 24 | tf_op jit(solution)/shard_map/psum | solution.py:29
  159.1 3.2 %sort.17 = (s32[256]{0:T(256)}, s32[256]{0:T(256)S(1)}) sort(s32[256]{0:T(256)S(1)} %compare_convert_fusion, s32[256]{0:T(256)S(1)} %iota.22), dimensions={0}, to_apply=%region_1.2 | sort | flops 2048 | bytes 4096 | tf_op jit(solution)/shard_map/jit(argsort)/sort | solution.py:52
  162.3 2.4 %psum.37 = f32[3]{0:T(128)S(1)} all-reduce(f32[3]{0:T(128)S(1)} %psum.36), channel_id=1, replica_groups=mesh['rows_0'=4,'rows_1'=4,'rows_2'=2,'cols_0'=4,'cols_1'=2] {'rows_2'}, use_global_device_ids=true, to_apply=%region_10.11 | all-reduce | flops 3 | bytes 24 | tf_op jit(solution)/shard_map/psum | solution.py:29
  164.8 17.0 %psum.38 = f32[3]{0:T(128)S(1)} all-reduce(f32[3]{0:T(128)S(1)} %psum.37), channel_id=1, replica_groups=mesh['rows_0'=4,'rows_1'=4,'rows_2'=2,'cols_0'=4,'cols_1'=2] {'cols_0'}, use_global_device_ids=true, to_apply=%region_11.12 | all-reduce | flops 3 | bytes 24 | tf_op jit(solution)/shard_map/psum | solution.py:29
  181.8 8.8 %psum.39 = f32[3]{0:T(128)S(1)} all-reduce(f32[3]{0:T(128)S(1)} %psum.38), channel_id=1, replica_groups=mesh['rows_0'=4,'rows_1'=4,'rows_2'=2,'cols_0'=4,'cols_1'=2] {'cols_1'}, use_global_device_ids=true, to_apply=%region_12.13 | all-reduce | flops 3 | bytes 24 | tf_op jit(solution)/shard_map/psum | solution.py:29
  190.6 0.5 broadcast_multiply_fusion
  191.1 3.0 %gather_fusion.1 = f32[8,8,2048]{2,1,0:T(8,128)} fusion(f32[32,8,2048]{2,1,0:T(8,128)} %all-to-all-done, s32[1024]{0:T(1024)S(1)} %pad_clamp_fusion), kind=kCustom, calls=%fused_computation.1 | custom fusion | bytes 1048608 | tf_op jit(solution)/shard_map/gather | solution.py:103
  (98 shorter events, 4.8 us)
Async XLA Ops:
  0.6 6.3 %copy-start.1 = (f32[64,2048]{1,0:T(8,128)S(1)}, f32[64,2048]{1,0:T(8,128)}, u32[]{:S(2)}) copy-start(f32[64,2048]{1,0:T(8,128)} %param.4) | copy-start | bytes 1572868
  1.6 12.3 %collective-permute-start = (f32[1,2048]{1,0:T(1,128)S(1)}, f32[1,2048]{1,0:T(1,128)S(1)}, u32[]{:S(2)}, u32[]{:S(2)}) collective-permute-start(f32[1,2048]{1,0:T(1,128)S(1)} %slice_bitcast_fusion.5), channel_id=1, source_target_pairs={{8,0},{16,8},{24,16},{32,24},{40,32},{48,40},{56,48},{64,56},{72,6... | collective-permute-start | bytes 24584 | tf_op jit(solution)/shard_map/ppermute | solution.py:24
  4.3 9.4 %collective-permute-start.1 = (f32[1,64]{1,0:T(1,128)S(1)}, f32[1,64]{1,0:T(1,128)S(1)}, u32[]{:S(2)}, u32[]{:S(2)}) collective-permute-start(f32[1,64]{1,0:T(1,128)S(1)} %bitcast.176), channel_id=1, source_target_pairs={{1,0},{2,1},{3,2},{4,3},{5,4},{6,5},{7,6},{9,8},{10,9},{11,10},{12... | collective-permute-start | bytes 776 | tf_op jit(solution)/shard_map/ppermute | solution.py:24
  5.6 1.8 copy-start.19
  7.1 7.3 %copy-start.3 = (f32[8,8,2047]{2,1,0:T(8,128)}, f32[8,8,2047]{2,1,0:T(8,128)S(1)}, u32[]{:S(2)}) copy-start(f32[8,8,2047]{2,1,0:T(8,128)S(1)} %fusion.46) | copy-start | bytes 1572100
  7.4 9.6 %copy-start.6 = (f32[64,2047]{1,0:T(8,128)}, f32[64,2047]{1,0:T(8,128)S(1)}, u32[]{:S(2)}) copy-start(f32[64,2047]{1,0:T(8,128)S(1)} %slice_subtract_fusion.5) | copy-start | bytes 1572100
  8.3 49.8 %copy-start.18 = (pred[8]{0:T(512)(128)(4,1)}, pred[8]{0:T(512)(128)(4,1)S(1)}, u32[]{:S(2)}) copy-start(pred[8]{0:T(512)(128)(4,1)S(1)} %fusion.39) | copy-start | bytes 28
  14.4 28.1 %copy-start.2 = (f32[8,8,2048]{2,1,0:T(8,128)}, f32[8,8,2048]{2,1,0:T(8,128)S(1)}, u32[]{:S(2)}) copy-start(f32[8,8,2048]{2,1,0:T(8,128)S(1)} %fusion.34) | copy-start | bytes 1572868
  14.5 12.8 %copy-start.16 = (f32[8,8,16,128]{3,2,1,0:T(8,128)S(1)}, f32[8,8,16,128]{3,2,1,0:T(8,128)}, u32[]{:S(2)}) copy-start(f32[8,8,16,128]{3,2,1,0:T(8,128)} %broadcast_bitcast_fusion) | copy-start | bytes 1572868
  14.5 12.7 %collective-permute-start.2 = (f32[1,2048]{1,0:T(1,128)S(1)}, f32[1,2048]{1,0:T(1,128)S(1)}, u32[]{:S(2)}, u32[]{:S(2)}) collective-permute-start(f32[1,2048]{1,0:T(1,128)S(1)} %slice_bitcast_fusion.4), channel_id=1, source_target_pairs={{0,8},{8,16},{16,24},{24,32},{32,40},{40,48},{48,56},{56,64},{64,7... | collective-permute-start | bytes 24584 | tf_op jit(solution)/shard_map/ppermute | solution.py:24
  17.1 9.9 %collective-permute-start.3 = (f32[1,64]{1,0:T(1,128)S(1)}, f32[1,64]{1,0:T(1,128)S(1)}, u32[]{:S(2)}, u32[]{:S(2)}) collective-permute-start(f32[1,64]{1,0:T(1,128)S(1)} %bitcast.185), channel_id=1, source_target_pairs={{0,1},{1,2},{2,3},{3,4},{4,5},{5,6},{6,7},{8,9},{9,10},{10,11},{11... | collective-permute-start | bytes 776 | tf_op jit(solution)/shard_map/ppermute | solution.py:24
  32.6 9.6 %collective-permute-start.5 = (f32[1,64]{1,0:T(1,128)S(1)}, f32[1,64]{1,0:T(1,128)S(1)}, u32[]{:S(2)}, u32[]{:S(2)}) collective-permute-start(f32[1,64]{1,0:T(1,128)S(1)} %bitcast.177), channel_id=1, source_target_pairs={{1,0},{2,1},{3,2},{4,3},{5,4},{6,5},{7,6},{9,8},{10,9},{11,10},{12... | collective-permute-start | bytes 776 | tf_op jit(solution)/shard_map/ppermute | solution.py:24
  34.0 8.4 %collective-permute-start.4 = (f32[1,2048]{1,0:T(1,128)S(1)}, f32[1,2048]{1,0:T(1,128)S(1)}, u32[]{:S(2)}, u32[]{:S(2)}) collective-permute-start(f32[1,2048]{1,0:T(1,128)S(1)} %slice_bitcast_fusion.3), channel_id=1, source_target_pairs={{8,0},{16,8},{24,16},{32,24},{40,32},{48,40},{56,48},{64,56},{72,6... | collective-permute-start | bytes 24584 | tf_op jit(solution)/shard_map/ppermute | solution.py:24
  42.3 5.1 %copy-start.9 = (f32[64,2048]{1,0:T(8,128)S(1)}, f32[64,2048]{1,0:T(8,128)}, u32[]{:S(2)}) copy-start(f32[64,2048]{1,0:T(8,128)} %get-tuple-element.19) | copy-start | bytes 1572868
  42.3 5.1 %copy-start.11 = (f32[64,2047]{1,0:T(8,128)S(1)}, f32[64,2047]{1,0:T(8,128)}, u32[]{:S(2)}) copy-start(f32[64,2047]{1,0:T(8,128)} %slice_subtract_fusion.2) | copy-start | bytes 1572100
  45.5 12.8 %copy-start.13 = (f32[8,8,2048]{2,1,0:T(8,128)}, f32[8,8,2048]{2,1,0:T(8,128)S(1)}, u32[]{:S(2)}) copy-start(f32[8,8,2048]{2,1,0:T(8,128)S(1)} %get-tuple-element.14) | copy-start | bytes 1572868
  45.5 11.3 %copy-start = (s32[256]{0:T(256)S(1)}, s32[256]{0:T(256)}, u32[]{:S(2)}) copy-start(s32[256]{0:T(256)} %param.7) | copy-start | bytes 3076
  45.5 12.7 %collective-permute-start.6 = (f32[1,2048]{1,0:T(1,128)S(1)}, f32[1,2048]{1,0:T(1,128)S(1)}, u32[]{:S(2)}, u32[]{:S(2)}) collective-permute-start(f32[1,2048]{1,0:T(1,128)S(1)} %slice_bitcast_fusion.2), channel_id=1, source_target_pairs={{0,8},{8,16},{16,24},{24,32},{32,40},{40,48},{48,56},{56,64},{64,7... | collective-permute-start | bytes 24584 | tf_op jit(solution)/shard_map/ppermute | solution.py:24
  48.1 10.0 %collective-permute-start.7 = (f32[1,64]{1,0:T(1,128)S(1)}, f32[1,64]{1,0:T(1,128)S(1)}, u32[]{:S(2)}, u32[]{:S(2)}) collective-permute-start(f32[1,64]{1,0:T(1,128)S(1)} %bitcast.182), channel_id=1, source_target_pairs={{0,1},{1,2},{2,3},{3,4},{4,5},{5,6},{6,7},{8,9},{9,10},{10,11},{11... | collective-permute-start | bytes 776 | tf_op jit(solution)/shard_map/ppermute | solution.py:24
  63.9 9.6 %collective-permute-start.9 = (f32[1,64]{1,0:T(1,128)S(1)}, f32[1,64]{1,0:T(1,128)S(1)}, u32[]{:S(2)}, u32[]{:S(2)}) collective-permute-start(f32[1,64]{1,0:T(1,128)S(1)} %bitcast.178), channel_id=1, source_target_pairs={{1,0},{2,1},{3,2},{4,3},{5,4},{6,5},{7,6},{9,8},{10,9},{11,10},{12... | collective-permute-start | bytes 776 | tf_op jit(solution)/shard_map/ppermute | solution.py:24
  65.3 8.4 %collective-permute-start.8 = (f32[1,2048]{1,0:T(1,128)S(1)}, f32[1,2048]{1,0:T(1,128)S(1)}, u32[]{:S(2)}, u32[]{:S(2)}) collective-permute-start(f32[1,2048]{1,0:T(1,128)S(1)} %slice_bitcast_fusion.1), channel_id=1, source_target_pairs={{8,0},{16,8},{24,16},{32,24},{40,32},{48,40},{56,48},{64,56},{72,6... | collective-permute-start | bytes 24584 | tf_op jit(solution)/shard_map/ppermute | solution.py:24
  73.6 4.6 %copy-start.8 = (f32[64,2048]{1,0:T(8,128)S(1)}, f32[64,2048]{1,0:T(8,128)}, u32[]{:S(2)}) copy-start(f32[64,2048]{1,0:T(8,128)} %get-tuple-element.13) | copy-start | bytes 1572868
  73.6 4.6 %copy-start.10 = (f32[64,2047]{1,0:T(8,128)S(1)}, f32[64,2047]{1,0:T(8,128)}, u32[]{:S(2)}) copy-start(f32[64,2047]{1,0:T(8,128)} %slice_subtract_fusion) | copy-start | bytes 1572100
  76.1 12.0 %copy-start.14 = (f32[8,8,2048]{2,1,0:T(8,128)}, f32[8,8,2048]{2,1,0:T(8,128)S(1)}, u32[]{:S(2)}) copy-start(f32[8,8,2048]{2,1,0:T(8,128)S(1)} %maximum_divide_fusion) | copy-start | bytes 1572868
  76.1 14.7 %copy-start.5 = (f32[64,2048]{1,0:T(8,128)S(1)}, f32[64,2048]{1,0:T(8,128)}, u32[]{:S(2)}) copy-start(f32[64,2048]{1,0:T(8,128)} %get-tuple-element.17) | copy-start | bytes 1572868
  76.2 13.9 %collective-permute-start.10 = (f32[1,2048]{1,0:T(1,128)S(1)}, f32[1,2048]{1,0:T(1,128)S(1)}, u32[]{:S(2)}, u32[]{:S(2)}) collective-permute-start(f32[1,2048]{1,0:T(1,128)S(1)} %slice_bitcast_fusion), channel_id=1, source_target_pairs={{0,8},{8,16},{16,24},{24,32},{32,40},{40,48},{48,56},{56,64},{64,7... | collective-permute-start | bytes 24584 | tf_op jit(solution)/shard_map/ppermute | solution.py:24
  78.7 9.5 %copy-start.15 = (f32[64,2048]{1,0:T(8,128)}, f32[64,2048]{1,0:T(8,128)S(1)}, u32[]{:S(2)}) copy-start(f32[64,2048]{1,0:T(8,128)S(1)} %fusion.30) | copy-start | bytes 1572868
  78.9 10.0 %collective-permute-start.11 = (f32[1,64]{1,0:T(1,128)S(1)}, f32[1,64]{1,0:T(1,128)S(1)}, u32[]{:S(2)}, u32[]{:S(2)}) collective-permute-start(f32[1,64]{1,0:T(1,128)S(1)} %bitcast.186), channel_id=1, source_target_pairs={{0,1},{1,2},{2,3},{3,4},{4,5},{5,6},{6,7},{8,9},{9,10},{10,11},{11... | collective-permute-start | bytes 776 | tf_op jit(solution)/shard_map/ppermute | solution.py:24
  88.9 0.5 copy-start.21
  95.1 1.5 copy-start.17
  95.1 1.5 copy-start.20
  99.1 10.0 %copy-start.4 = (f32[8,8,2047]{2,1,0:T(8,128)S(1)}, f32[8,8,2047]{2,1,0:T(8,128)}, u32[]{:S(2)}) copy-start(f32[8,8,2047]{2,1,0:T(8,128)} %copy-done.3) | copy-start | bytes 1572100
  99.2 10.0 %copy-start.7 = (f32[8,8,2047]{2,1,0:T(8,128)S(1)}, f32[8,8,2047]{2,1,0:T(8,128)}, u32[]{:S(2)}) copy-start(f32[8,8,2047]{2,1,0:T(8,128)} %fusion.45) | copy-start | bytes 1572100
  99.2 10.1 %copy-start.12 = (f32[8,8,2047]{2,1,0:T(8,128)S(1)}, f32[8,8,2047]{2,1,0:T(8,128)}, u32[]{:S(2)}) copy-start(f32[8,8,2047]{2,1,0:T(8,128)} %fusion.44) | copy-start | bytes 1572100
  99.2 91.9 %all-to-all-start = ((f32[32,8,2048]{2,1,0:T(8,128)}), f32[32,8,2048]{2,1,0:T(8,128)}, u32[]{:S(2)}, u32[]{:S(2)}) async-start(f32[32,8,2048]{2,1,0:T(8,128)} %scatter_fusion), calls=%async_computation | async-start | bytes 4194304 | tf_op jit(solution)/shard_map/all_to_all | solution.py:103
where the time goes:
time: 195 us; the launch traced here: 194 us
  blocking collectives  72.8 us (37%)
  starting transfers between devices  53.5 us (27%)
  other arithmetic  31.2 us (16%)
  waiting for transfers between devices  18.6 us (10%)
  local copies, waits for them, and re-layouts  13 us (7%)
  between operations  4.99 us (3%)
    psum x5, blocking collectives, over_axes(): array = lax.psum(array, axis)  72.8 us
    ppermute x12, starting transfers between devices, passed_along(): return lax.ppermute(block, axis, route)  43.5 us
    ppermute x12, waiting for transfers between devices, passed_along(): return lax.ppermute(block, axis, route)  18.6 us
    all_to_all x1, starting transfers between devices, per_device(): lax.all_to_all(empty.at[targets].set(primal.reshape(blocks_here, BR, widt...  10 us
    sub x2, other arithmetic, per_device(): extrap = 2.0 * updated - primal  6.69 us
    div x3, other arithmetic, per_device(): dual_rows = trial_rows / shrink  5.54 us
    reduce_sum x1, other arithmetic, per_device(): jnp.sum(0.5 * fidelity * misfit * misfit)  4.3 us
  transfers between devices with their start and end apart: 13, of which 6 were waited for; matrix products, arithmetic and copies ran while one was open for 7% of the time, Pallas kernels for 0%

commit v1 on v0

v1 whole, which is shorter than its diff:
```python
import functools

import jax
import jax.numpy as jnp
from jax import lax
from jax.experimental import pallas as pl
from jax.experimental.pallas import tpu as pltpu
from jax.sharding import PartitionSpec as P

BR = 8
TW = 128
ITERS = 3
HALF = 4

fidelity_scale = 0.25
tau_step = 0.35
sigma_step = 0.35
tv_weight = 0.3

MESH = pl.DeviceIdType.MESH


def kernel(
    n_rows, n_cols, blocks, tiles, pixel_total,
    image_hbm, mask_hbm, weight_ref, owner_ref,
    out_hbm, objective_ref,
    img, fid, gain, bias, prim, ext, dual_r, dual_c, mask_v,
    row_msg, row_got, col_msg, col_got, corner_got,
    staged, spread, sorted_, gathered, out_v,
    order_v, order_s, acc, part_src, part_rows, part_src_c, part_cols,
    load_sem, order_sem, halo_send, halo_recv,
    send1, recv1, send2, recv2, psend, precv, csend, crecv, out_sem,
):
    width = tiles * TW
    ring = width + TW
    r = lax.axis_index("rows")
    c = lax.axis_index("cols")
    up, down = lax.rem(r + n_rows - 1, n_rows), lax.rem(r + 1, n_rows)
    left, right = lax.rem(c + n_cols - 1, n_cols), lax.rem(c + 1, n_cols)

    load_image = pltpu.make_async_copy(image_hbm, img.at[pl.ds(0, blocks), :, pl.ds(0, width)], load_sem.at[0])
    load_mask = pltpu.make_async_copy(mask_hbm, mask_v, load_sem.at[1])
    load_image.start()
    load_mask.start()

    barrier = pltpu.get_barrier_semaphore()

    def greet(row, col):
        pl.semaphore_signal(barrier, inc=1, device_id=(row, col), device_id_type=MESH)

    @pl.loop(1, n_cols)
    def _(j):
        greet(r, lax.rem(c + j, n_cols))

    for row in (up, down):
        for col in (left, right):
            greet(row, col)

    @pl.loop(1, n_rows)
    def _(j):
        greet(lax.rem(r + j, n_rows), c)

    total = n_rows * blocks
    own = jnp.broadcast_to(owner_ref[...], (total, total))
    before = lax.broadcasted_iota(jnp.int32, (total, total), 0)
    after = lax.broadcasted_iota(jnp.int32, (total, total), 1)
    same = (own == own.T) & (before < after)
    rank = jnp.sum(jnp.where(same, 1, 0), axis=0, keepdims=True)
    place = jnp.broadcast_to(owner_ref[...] * blocks + rank, (total, total)).T
    order_v[...] = jnp.sum(jnp.where(place == after, before, 0), axis=0, keepdims=True)
    to_scalars = pltpu.make_async_copy(order_v, order_s, order_sem)
    to_scalars.start()

    load_image.wait()
    load_mask.wait()

    sub = lax.broadcasted_iota(jnp.int32, (BR, ring), 0)
    lane = lax.broadcasted_iota(jnp.int32, (BR, ring), 1)
    sub_w = lax.broadcasted_iota(jnp.int32, (BR, width), 0)

    @pl.loop(0, blocks)
    def _(i):
        weights = jnp.concatenate(
            [jnp.full((BR, TW), weight_ref[i, t].astype(jnp.float32) * fidelity_scale) for t in range(tiles)], axis=1
        )
        fid[i, :, pl.ds(0, width)] = weights * (1 - mask_v[i]).astype(jnp.float32)

    last = blocks - 1
    row_msg[0] = jnp.where(sub_w < HALF, img[0, :, pl.ds(0, width)], pltpu.roll(fid[0, :, pl.ds(0, width)], HALF, 0))
    row_msg[1] = jnp.where(
        sub_w >= HALF, img[last, :, pl.ds(0, width)], pltpu.roll(fid[last, :, pl.ds(0, width)], HALF, 0)
    )
    rows_here = blocks * BR
    for side, start in ((0, 0), (1, width - TW)):
        both = jnp.concatenate(
            [
                img[pl.ds(0, blocks), :, pl.ds(start, TW)].reshape(rows_here, TW),
                fid[pl.ds(0, blocks), :, pl.ds(start, TW)].reshape(rows_here, TW),
            ],
            axis=0,
        ).T
        col_msg[side] = both[:BR] if side == 0 else both[TW - BR :]

    pl.semaphore_wait(barrier, n_rows - 1 + n_cols - 1 + 4)

    first_tile, last_tile = pl.ds(0, TW), pl.ds(width - TW, TW)
    messages = (
        (row_msg.at[0], row_got.at[0], up, c),
        (row_msg.at[1], row_got.at[1], down, c),
        (col_msg.at[0], col_got.at[0], r, left),
        (col_msg.at[1], col_got.at[1], r, right),
        (row_msg.at[0, :, first_tile], corner_got.at[0], up, left),
        (row_msg.at[0, :, last_tile], corner_got.at[1], up, right),
        (row_msg.at[1, :, first_tile], corner_got.at[2], down, left),
        (row_msg.at[1, :, last_tile], corner_got.at[3], down, right),
    )
    halos = [
        pltpu.make_async_remote_copy(
            src_ref=src, dst_ref=dst, send_sem=halo_send.at[k], recv_sem=halo_recv.at[k],
            device_id=(row, col), device_id_type=MESH,
        )
        for k, (src, dst, row, col) in enumerate(messages)
    ]
    for k in (2, 3, 4, 5, 6, 7, 0, 1):
        halos[k].start()
    for halo in halos:
        halo.wait_recv()

    below, above = row_got[0], row_got[1]
    img[blocks, :, pl.ds(0, width)] = jnp.where(sub_w < HALF, below, above)
    fid[blocks, :, pl.ds(0, width)] = pltpu.roll(jnp.where(sub_w < HALF, above, below), HALF, 0)
    sides = jnp.concatenate([col_got[0], jnp.zeros((TW - 2 * BR, TW), jnp.float32), col_got[1]], axis=0).T
    img[pl.ds(0, blocks), :, pl.ds(width, TW)] = sides[:rows_here].reshape(blocks, BR, TW)
    fid[pl.ds(0, blocks), :, pl.ds(width, TW)] = sides[rows_here:].reshape(blocks, BR, TW)
    sub_t = lax.broadcasted_iota(jnp.int32, (BR, TW), 0)
    lane_t = lax.broadcasted_iota(jnp.int32, (BR, TW), 1)
    low = jnp.where(lane_t < TW // 2, corner_got[0], corner_got[1])
    high = jnp.where(lane_t < TW // 2, corner_got[2], corner_got[3])
    img[blocks, :, pl.ds(width, TW)] = jnp.where(sub_t < HALF, low, high)
    fid[blocks, :, pl.ds(width, TW)] = pltpu.roll(jnp.where(sub_t < HALF, high, low), HALF, 0)

    @pl.loop(0, blocks + 1)
    def _(i):
        f = fid[i] * tau_step
        g = 1.0 / (1.0 + f)
        v = img[i]
        gain[i] = g
        bias[i] = f * v * g
        prim[i] = v
        ext[i] = v
        zero = jnp.zeros_like(v)
        dual_r[i] = zero
        dual_c[i] = zero

    edge_col = jnp.where(c == n_cols - 1, width - 1, jnp.where(c == 0, ring - 1, -1))

    def folded(x):
        parts = [x[:, t * TW : (t + 1) * TW] for t in range(tiles)]
        while len(parts) > 1:
            parts = [a + b for a, b in zip(parts[::2], parts[1::2])]
        return parts[0]

    def dual_step(i, following, edge_row):
        e = ext[i]
        lower = jnp.where(sub == BR - 1, pltpu.roll(ext[following], BR - 1, 0), pltpu.roll(e, BR - 1, 0))
        grad_r = jnp.where(sub == edge_row, 0.0, lower - e)
        grad_c = jnp.where(lane == edge_col, 0.0, pltpu.roll(e, ring - 1, 1) - e)
        trial_r = dual_r[i] + sigma_step * grad_r
        trial_c = dual_c[i] + sigma_step * grad_c
        scale = jnp.minimum(1.0, tv_weight * lax.rsqrt(trial_r * trial_r + trial_c * trial_c))
        dual_r[i] = trial_r * scale
        dual_c[i] = trial_c * scale
        return grad_r, grad_c

    def primal_step(i, previous):
        dr, dc, p = dual_r[i], dual_c[i], prim[i]
        upper = jnp.where(sub == 0, pltpu.roll(dual_r[previous], 1, 0), pltpu.roll(dr, 1, 0))
        div = dr - upper + (dc - pltpu.roll(dc, 1, 1))
        updated = (p + tau_step * div) * gain[i] + bias[i]
        ext[i] = 2.0 * updated - p
        prim[i] = updated
        return updated

    @pl.loop(0, ITERS)
    def _(step):
        dual_step(blocks, 0, jnp.where(r == 0, BR - 1, BR))

        def body(i, partial):
            edge_row = jnp.where((i == last) & (r == n_rows - 1), BR - 1, BR)
            grad_r, grad_c = dual_step(i, i + 1, edge_row)
            partial += tv_weight * folded(jnp.sqrt(grad_r * grad_r + grad_c * grad_c))
            misfit = primal_step(i, jnp.where(i == 0, blocks, i - 1)) - img[i]
            return partial + 0.5 * folded(fid[i] * misfit * misfit)

        acc[step] = lax.fori_loop(0, blocks, body, jnp.zeros((BR, TW), jnp.float32))
        primal_step(blocks, last)

    lane_1 = lax.broadcasted_iota(jnp.int32, (1, TW), 1)
    sums = jnp.zeros((1, TW), jnp.float32)
    for step in range(ITERS):
        line = jnp.sum(acc[step], axis=0, keepdims=True)
        sums = jnp.where(lane_1 == step, jnp.sum(line, axis=1, keepdims=True), sums)
    part_src[...] = sums
    part_rows[r] = sums

    @pl.loop(0, blocks)
    def _(i):
        p = prim[i]
        for t in range(tiles):
            tile = p[:, t * TW : (t + 1) * TW]
            staged[2 * t, i] = tile[:HALF]
            staged[2 * t + 1, i] = tile[HALF:]

    def spread_to(m):
        return pltpu.make_async_remote_copy(
            src_ref=staged.at[m], dst_ref=spread.at[r], send_sem=send1, recv_sem=recv1,
            device_id=(m, c), device_id_type=MESH,
        )

    def part_to(m):
        return pltpu.make_async_remote_copy(
            src_ref=part_src, dst_ref=part_rows.at[r], send_sem=psend, recv_sem=precv,
            device_id=(m, c), device_id_type=MESH,
        )

    @pl.loop(1, n_rows)
    def _(j):
        spread_to(lax.rem(r + j, n_rows)).start()

    @pl.loop(1, n_rows)
    def _(j):
        part_to(lax.rem(r + j, n_rows)).start()

    spread[r] = staged[r]
    to_scalars.wait()
    peers = pl.ds(0, n_rows - 1)
    all_spread = pltpu.make_async_remote_copy(
        src_ref=staged.at[peers], dst_ref=spread.at[peers], send_sem=send1, recv_sem=recv1,
        device_id=(up, c), device_id_type=MESH,
    )
    all_spread.wait_recv()

    def collect_to(d):
        return pltpu.make_async_remote_copy(
            src_ref=sorted_.at[d], dst_ref=gathered.at[r], send_sem=send2, recv_sem=recv2,
            device_id=(d, c), device_id_type=MESH,
        )

    def sort_for(d):
        for k in range(blocks):
            b = order_s[0, d * blocks + k]
            sorted_[d, k] = spread[b // blocks, lax.rem(b, blocks)]

    sort_for(lax.rem(r + 1, n_rows))

    @pl.loop(2, n_rows)
    def _(j):
        sort_for(lax.rem(r + j, n_rows))
        collect_to(lax.rem(r + j - 1, n_rows)).start()

    sort_for(r)
    collect_to(up).start()
    gathered[r] = sorted_[r]

    all_parts = pltpu.make_async_remote_copy(
        src_ref=part_rows.at[peers], dst_ref=part_rows.at[peers], send_sem=psend, recv_sem=precv,
        device_id=(up, c), device_id_type=MESH,
    )
    all_parts.wait_recv()
    here = part_rows[0]
    for s in range(1, n_rows):
        here = here + part_rows[s]
    part_src_c[...] = here
    part_cols[c] = here

    def part_across(col):
        return pltpu.make_async_remote_copy(
            src_ref=part_src_c, dst_ref=part_cols.at[c], send_sem=csend, recv_sem=crecv,
            device_id=(r, col), device_id_type=MESH,
        )

    @pl.loop(1, n_cols)
    def _(j):
        part_across(lax.rem(c + j, n_cols)).start()

    col_peers = pl.ds(0, n_cols - 1)
    all_cols = pltpu.make_async_remote_copy(
        src_ref=part_cols.at[col_peers], dst_ref=part_cols.at[col_peers], send_sem=csend, recv_sem=crecv,
        device_id=(r, left), device_id_type=MESH,
    )
    all_cols.wait_recv()
    everywhere = part_cols[0]
    for s in range(1, n_cols):
        everywhere = everywhere + part_cols[s]
    for step in range(ITERS):
        objective_ref[step] = jnp.sum(jnp.where(lane_1 == step, everywhere, 0.0)) / pixel_total

    all_collected = pltpu.make_async_remote_copy(
        src_ref=sorted_.at[peers], dst_ref=gathered.at[peers], send_sem=send2, recv_sem=recv2,
        device_id=(up, c), device_id_type=MESH,
    )
    all_collected.wait_recv()

    @pl.loop(0, blocks)
    def _(k):
        for t in range(tiles):
            out_v[k, :, pl.ds(t * TW, TW)] = jnp.concatenate([gathered[2 * t, k], gathered[2 * t + 1, k]], axis=0)

    store = pltpu.make_async_copy(out_v, out_hbm, out_sem)
    store.start()
    for halo in halos:
        halo.wait_send()
    all_spread.wait_send()
    all_parts.wait_send()
    all_cols.wait_send()
    all_collected.wait_send()
    store.wait()


def per_device(n_rows, n_cols, image, cloud_mask, tile_weight, owner):
    rows_here, width = image.shape
    blocks = rows_here // BR
    tiles = width // TW
    pixel_total = float(n_rows * n_cols * rows_here * width)
    f32 = jnp.float32
    ringed = pltpu.VMEM((blocks + 1, BR, width + TW), f32)
    pieces = pltpu.VMEM((n_rows, blocks, HALF, TW), f32)
    dma = pltpu.SemaphoreType.DMA
    scratch = (
        [ringed] * 8
        + [
            pltpu.VMEM((blocks, BR, width), jnp.int32),
            pltpu.VMEM((2, BR, width), f32),
            pltpu.VMEM((2, BR, width), f32),
            pltpu.VMEM((2, BR, TW), f32),
            pltpu.VMEM((2, BR, TW), f32),
            pltpu.VMEM((4, BR, TW), f32),
        ]
        + [pieces] * 4
        + [
            pltpu.VMEM((blocks, BR, width), f32),
            pltpu.VMEM((1, n_rows * blocks), jnp.int32),
            pltpu.SMEM((1, n_rows * blocks), jnp.int32),
            pltpu.VMEM((ITERS, BR, TW), f32),
            pltpu.VMEM((1, TW), f32),
            pltpu.VMEM((n_rows, 1, TW), f32),
            pltpu.VMEM((1, TW), f32),
            pltpu.VMEM((n_cols, 1, TW), f32),
            dma((2,)), dma, dma((8,)), dma((8,)),
            dma, dma, dma, dma, dma, dma, dma, dma, dma,
        ]
    )
    vmem, smem, hbm = (pl.BlockSpec(memory_space=s) for s in (pltpu.VMEM, pltpu.SMEM, pl.ANY))
    out, objective = pl.pallas_call(
        functools.partial(kernel, n_rows, n_cols, blocks, tiles, pixel_total),
        out_shape=(
            jax.ShapeDtypeStruct((blocks, BR, width), f32),
            jax.ShapeDtypeStruct((ITERS,), f32),
        ),
        in_specs=[hbm, hbm, smem, vmem],
        out_specs=(hbm, smem),
        scratch_shapes=scratch,
        compiler_params=pltpu.CompilerParams(collective_id=0, has_side_effects=True),
    )(
        image.reshape(blocks, BR, width),
        cloud_mask.reshape(blocks, BR, width),
        tile_weight,
        owner.reshape(1, -1),
    )
    return out.reshape(rows_here, width), objective


def solution(mesh):
    placed = (P("rows", "cols"), P("rows", "cols"), P("rows", "cols"), P())
    return jax.shard_map(
        functools.partial(per_device, mesh.shape["rows"], mesh.shape["cols"]),
        mesh=mesh, in_specs=placed, out_specs=(P("rows", "cols"), P()), check_vma=False,
    )
```

time: 195 us -> 55.7 us (0.29)
  the two profiles are of different devices: /device:TPU:70 before, /device:TPU:1 now
where the time goes in v1:
time: 55.7 us; the launch traced here: 55.6 us
  Pallas kernels  52.5 us (94%)
  local copies, waits for them, and re-layouts  2.39 us (4%)
  between operations  0.65 us (1%)
    pallas_call x1, Pallas kernels, per_device(): pl.pallas_call(functools.partial(kernel, n_rows, n_cols, blocks, tiles, p...  52.5 us
    unnamed x4, local copies, waits for them, and re-layouts  2.39 us

profile of v1, /device:TPU:1, one launch (start us, length us, event | category | flops | bytes accessed | tf_op | source)
XLA Modules:
  0.0 55.6 jit_solution(17376751628063228857)
XLA Ops:
  0.6 52.5 %shard_map.59 = (f32[8,8,2048]{2,1,0:T(8,128)}, f32[3]{0:T(128)}) custom-call(f32[8,8,2048]{2,1,0:T(8,128)} %bitcast.4, s32[8,8,2048]{2,1,0:T(8,128)} %bitcast.5, s32[8,16]{1,0:T(8,128)} %weight_ref.1, s32[1,256]{1,0:T(1,128)} %bitcast.7), custom_call_target="tpu_custom_call" | custom-call | tf_op jit(solution)/shard_map/pallas_call | solution.py:354
  53.2 0.0 copy-start
  53.2 1.9 %copy.8 = f32[64,2048]{1,0:T(8,128)} copy(f32[64,2048]{1,0:T(8,128)} %bitcast.6) | data formatting | bytes 1048576
  55.0 0.0 copy-done
  55.0 0.5 copy.9
Async XLA Ops:
  53.2 1.9 %copy-start = (f32[3]{0:T(128)S(1)}, f32[3]{0:T(128)}, u32[]{:S(2)}) copy-start(f32[3]{0:T(128)} %get-tuple-element.9) | copy-start | bytes 40

commit v2 on v1

--- a/solution.py
+++ b/solution.py
@@ -24,7 +24,8 @@
     n_rows, n_cols, blocks, tiles, pixel_total,
     image_hbm, mask_hbm, weight_ref, owner_ref,
     out_hbm, objective_ref,
-    img, fid, gain, bias, prim, ext, dual_r, dual_c, mask_v,
+    img, fid, gain, bias, prim, ext, dual_r, dual_c,
+    strip_prim, strip_ext, strip_r, strip_c, side_prim, side_ext, side_r, side_c, mask_v,
     row_msg, row_got, col_msg, col_got, corner_got,
     staged, spread, sorted_, gathered, out_v,
     order_v, order_s, acc, part_src, part_rows, part_src_c, part_cols,
@@ -74,18 +75,27 @@
     load_image.wait()
     load_mask.wait()
 
-    sub = lax.broadcasted_iota(jnp.int32, (BR, ring), 0)
-    lane = lax.broadcasted_iota(jnp.int32, (BR, ring), 1)
+    sub = lax.broadcasted_iota(jnp.int32, (BR, TW), 0)
+    lane = lax.broadcasted_iota(jnp.int32, (BR, TW), 1)
     sub_w = lax.broadcasted_iota(jnp.int32, (BR, width), 0)
+    last, last_t = blocks - 1, tiles - 1
+
+    def at(t):
+        return pl.ds(t * TW if isinstance(t, int) else pl.multiple_of(t * TW, TW), TW)
+
+    def coefficients(i, where):
+        f = fid[i, :, where] * tau_step
+        g = 1.0 / (1.0 + f)
+        gain[i, :, where] = g
+        bias[i, :, where] = f * img[i, :, where] * g
 
     @pl.loop(0, blocks)
     def _(i):
-        weights = jnp.concatenate(
-            [jnp.full((BR, TW), weight_ref[i, t].astype(jnp.float32) * fidelity_scale) for t in range(tiles)], axis=1
-        )
-        fid[i, :, pl.ds(0, width)] = weights * (1 - mask_v[i]).astype(jnp.float32)
-
-    last = blocks - 1
+        for t in range(tiles):
+            weight = weight_ref[i, t].astype(jnp.float32) * fidelity_scale
+            fid[i, :, at(t)] = weight * (1 - mask_v[i, :, at(t)]).astype(jnp.float32)
+            coefficients(i, at(t))
+
     row_msg[0] = jnp.where(sub_w < HALF, img[0, :, pl.ds(0, width)], pltpu.roll(fid[0, :, pl.ds(0, width)], HALF, 0))
     row_msg[1] = jnp.where(
         sub_w >= HALF, img[last, :, pl.ds(0, width)], pltpu.roll(fid[last, :, pl.ds(0, width)], HALF, 0)
@@ -101,6 +111,67 @@
         ).T
         col_msg[side] = both[:BR] if side == 0 else both[TW - BR :]
 
+    def dual_update(e, e_right, e_below, dr, dc, no_row=None, no_col=None):
+        grad_r = pltpu.roll(jnp.where(sub == 0, e_below, e), BR - 1, 0) - e
+        grad_c = pltpu.roll(jnp.where(lane == 0, e_right, e), TW - 1, 1) - e
+        if no_row is not None:
+            grad_r = jnp.where(sub == no_row, 0.0, grad_r)
+        if no_col is not None:
+            grad_c = jnp.where(lane == no_col, 0.0, grad_c)
+        trial_r = sigma_step * grad_r
+        trial_c = sigma_step * grad_c
+        if dr is not None:
+            trial_r, trial_c = dr + trial_r, dc + trial_c
+        scale = jnp.minimum(1.0, tv_weight * lax.rsqrt(trial_r * trial_r + trial_c * trial_c))
+        return trial_r * scale, trial_c * scale, jnp.sqrt(grad_r * grad_r + grad_c * grad_c)
+
+    def primal_update(p, dr, dc, dr_above, dc_left, g, b):
+        upper = pltpu.roll(jnp.where(sub == BR - 1, dr_above, dr), 1, 0)
+        before = pltpu.roll(jnp.where(lane == TW - 1, dc_left, dc), 1, 1)
+        return (p + tau_step * ((dr - upper) + (dc - before))) * g + b
+
+    def loss(variation, f, misfit):
+        return tv_weight * variation + 0.5 * f * (misfit * misfit)
+
+    for step in range(ITERS):
+        old = img if step == 0 else ext
+        old_prim = img if step == 0 else prim
+
+        def body(i, partial, step=step, old=old, old_prim=old_prim):
+            following, previous = jnp.minimum(i + 1, last), jnp.maximum(i - 1, 0)
+            row = jnp.zeros((BR, TW), jnp.float32)
+            e = old[i, :, at(0)]
+            dc_left = None
+            for t in range(tiles):
+                e_right = old[i, :, at(min(t + 1, last_t))]
+                dr, dc = (None, None) if step == 0 else (dual_r[i, :, at(t)], dual_c[i, :, at(t)])
+                dr, dc, variation = dual_update(e, e_right, old[following, :, at(t)], dr, dc)
+                dual_r[i, :, at(t)] = dr
+                dual_c[i, :, at(t)] = dc
+                p = old_prim[i, :, at(t)]
+                updated = primal_update(
+                    p, dr, dc, dual_r[previous, :, at(t)], dc if t == 0 else dc_left, gain[i, :, at(t)], bias[i, :, at(t)]
+                )
+                dc_left = dc
+                if step < ITERS - 1:
+                    ext[i, :, at(t)] = 2.0 * updated - p
+                else:
+                    staged[2 * t, i] = updated[:HALF]
+                    staged[2 * t + 1, i] = updated[HALF:]
+                prim[i, :, at(t)] = updated
+                term = loss(variation, fid[i, :, at(t)], updated - img[i, :, at(t)])
+                if t == 0:
+                    term = jnp.where(lane >= TW // 2, term, 0.0)
+                if t == last_t:
+                    term = jnp.where(lane < TW // 2, term, 0.0)
+                row = row + term
+                e = e_right
+            first = jnp.where(i == 0, HALF, 0)
+            end = jnp.where(i == last, HALF, BR)
+            return partial + jnp.where((sub >= first) & (sub < end), row, 0.0)
+
+        acc[step] = lax.fori_loop(0, blocks, body, jnp.zeros((BR, TW), jnp.float32))
+
     pl.semaphore_wait(barrier, n_rows - 1 + n_cols - 1 + 4)
 
     first_tile, last_tile = pl.ds(0, TW), pl.ds(width - TW, TW)
@@ -123,6 +194,22 @@
     ]
     for k in (2, 3, 4, 5, 6, 7, 0, 1):
         halos[k].start()
+
+    def spread_to(m, start, size):
+        piece = pl.ds(start, size)
+        return pltpu.make_async_remote_copy(
+            src_ref=staged.at[m, piece], dst_ref=spread.at[r, piece], send_sem=send1, recv_sem=recv1,
+            device_id=(m, c), device_id_type=MESH,
+        )
+
+    @pl.loop(1, n_rows)
+    def _(j):
+        m = lax.rem(r + j, n_rows)
+
+        @pl.when((m >= 2) & (m < n_rows - 2))
+        def _():
+            spread_to(m, 1 - lax.rem(m, 2), last).start()
+
     for halo in halos:
         halo.wait_recv()
 
@@ -132,68 +219,109 @@
     sides = jnp.concatenate([col_got[0], jnp.zeros((TW - 2 * BR, TW), jnp.float32), col_got[1]], axis=0).T
     img[pl.ds(0, blocks), :, pl.ds(width, TW)] = sides[:rows_here].reshape(blocks, BR, TW)
     fid[pl.ds(0, blocks), :, pl.ds(width, TW)] = sides[rows_here:].reshape(blocks, BR, TW)
-    sub_t = lax.broadcasted_iota(jnp.int32, (BR, TW), 0)
-    lane_t = lax.broadcasted_iota(jnp.int32, (BR, TW), 1)
-    low = jnp.where(lane_t < TW // 2, corner_got[0], corner_got[1])
-    high = jnp.where(lane_t < TW // 2, corner_got[2], corner_got[3])
-    img[blocks, :, pl.ds(width, TW)] = jnp.where(sub_t < HALF, low, high)
-    fid[blocks, :, pl.ds(width, TW)] = pltpu.roll(jnp.where(sub_t < HALF, high, low), HALF, 0)
-
-    @pl.loop(0, blocks + 1)
-    def _(i):
-        f = fid[i] * tau_step
-        g = 1.0 / (1.0 + f)
-        v = img[i]
-        gain[i] = g
-        bias[i] = f * v * g
-        prim[i] = v
-        ext[i] = v
-        zero = jnp.zeros_like(v)
-        dual_r[i] = zero
-        dual_c[i] = zero
-
-    edge_col = jnp.where(c == n_cols - 1, width - 1, jnp.where(c == 0, ring - 1, -1))
-
-    def folded(x):
-        parts = [x[:, t * TW : (t + 1) * TW] for t in range(tiles)]
-        while len(parts) > 1:
-            parts = [a + b for a, b in zip(parts[::2], parts[1::2])]
-        return parts[0]
-
-    def dual_step(i, following, edge_row):
-        e = ext[i]
-        lower = jnp.where(sub == BR - 1, pltpu.roll(ext[following], BR - 1, 0), pltpu.roll(e, BR - 1, 0))
-        grad_r = jnp.where(sub == edge_row, 0.0, lower - e)
-        grad_c = jnp.where(lane == edge_col, 0.0, pltpu.roll(e, ring - 1, 1) - e)
-        trial_r = dual_r[i] + sigma_step * grad_r
-        trial_c = dual_c[i] + sigma_step * grad_c
-        scale = jnp.minimum(1.0, tv_weight * lax.rsqrt(trial_r * trial_r + trial_c * trial_c))
-        dual_r[i] = trial_r * scale
-        dual_c[i] = trial_c * scale
-        return grad_r, grad_c
-
-    def primal_step(i, previous):
-        dr, dc, p = dual_r[i], dual_c[i], prim[i]
-        upper = jnp.where(sub == 0, pltpu.roll(dual_r[previous], 1, 0), pltpu.roll(dr, 1, 0))
-        div = dr - upper + (dc - pltpu.roll(dc, 1, 1))
-        updated = (p + tau_step * div) * gain[i] + bias[i]
-        ext[i] = 2.0 * updated - p
-        prim[i] = updated
-        return updated
-
-    @pl.loop(0, ITERS)
-    def _(step):
-        dual_step(blocks, 0, jnp.where(r == 0, BR - 1, BR))
-
-        def body(i, partial):
-            edge_row = jnp.where((i == last) & (r == n_rows - 1), BR - 1, BR)
-            grad_r, grad_c = dual_step(i, i + 1, edge_row)
-            partial += tv_weight * folded(jnp.sqrt(grad_r * grad_r + grad_c * grad_c))
-            misfit = primal_step(i, jnp.where(i == 0, blocks, i - 1)) - img[i]
-            return partial + 0.5 * folded(fid[i] * misfit * misfit)
-
-        acc[step] = lax.fori_loop(0, blocks, body, jnp.zeros((BR, TW), jnp.float32))
-        primal_step(blocks, last)
+    low = jnp.where(lane < TW // 2, corner_got[0], corner_got[1])
+    high = jnp.where(lane < TW // 2, corner_got[2], corner_got[3])
+    img[blocks, :, pl.ds(width, TW)] = jnp.where(sub < HALF, low, high)
+    fid[blocks, :, pl.ds(width, TW)] = pltpu.roll(jnp.where(sub < HALF, high, low), HALF, 0)
+
+    coefficients(blocks, pl.ds(0, ring))
+    for i in range(blocks):
+        coefficients(i, at(tiles))
+
+    zero = jnp.zeros((BR, TW), jnp.float32)
+
+    rows_of = (last, blocks, 0)
+    no_rows = (jnp.where(r == n_rows - 1, BR - 1, BR), jnp.where(r == 0, BR - 1, BR), None)
+    group = 4
+
+    for step in range(ITERS):
+
+        def strip_body(q, partial, step=step):
+            def source(refs, k, t):
+                return img[rows_of[k], :, at(t)] if step == 0 else refs[k, :, at(t)]
+
+            for n in range(group):
+                t = q * group + n
+                before, after = jnp.maximum(t - 1, 0), jnp.minimum(t + 1, last_t)
+                e = [source(strip_ext, k, t) for k in range(3)]
+                duals = []
+                for k in range(3):
+                    dr, dc = (None, None) if step == 0 else (strip_r[k, :, at(t)], strip_c[k, :, at(t)])
+                    duals.append(
+                        dual_update(e[k], source(strip_ext, k, after), e[(k + 1) % 3], dr, dc, no_row=no_rows[k])
+                    )
+                for k in range(3):
+                    dr, dc, variation = duals[k]
+                    dc_left = strip_c[k, :, at(before)] if n or step else jnp.where(q == 0, dc, strip_c[k, :, at(before)])
+                    strip_r[k, :, at(t)] = dr
+                    strip_c[k, :, at(t)] = dc
+                    p = source(strip_prim, k, t)
+                    i = rows_of[k]
+                    updated = primal_update(
+                        p, dr, dc, duals[(k + 2) % 3][0], dc_left, gain[i, :, at(t)], bias[i, :, at(t)]
+                    )
+                    if step < ITERS - 1:
+                        strip_ext[k, :, at(t)] = 2.0 * updated - p
+                    strip_prim[k, :, at(t)] = updated
+                    if k != 1:
+                        term = loss(variation, fid[i, :, at(t)], updated - img[i, :, at(t)])
+                        keep = sub < HALF if k == 2 else sub >= HALF
+                        if n == 0:
+                            keep = keep & (lane >= jnp.where(q == 0, TW // 2, 0))
+                        if n == group - 1:
+                            keep = keep & (lane < jnp.where(t == last_t, TW // 2, TW))
+                        partial = partial + jnp.where(keep, term, 0.0)
+            return partial
+
+        acc[step] = lax.fori_loop(0, tiles // group, strip_body, acc[step])
+
+    cols_of = (last_t, tiles, 0)
+    no_cols = (jnp.where(c == n_cols - 1, TW - 1, TW), jnp.where(c == 0, TW - 1, TW), None)
+    for step in range(ITERS):
+        partial = acc[step]
+        e = [
+            [img[i, :, at(cols_of[k])] if step == 0 else side_ext[i, :, at(k)] for k in range(3)]
+            for i in range(blocks + 1)
+        ]
+        variations = {}
+        for i in range(blocks + 1):
+            no_row = no_rows[0] if i == last else no_rows[1] if i == blocks else None
+            for k in range(3):
+                dr, dc = (None, None) if step == 0 else (side_r[i, :, at(k)], side_c[i, :, at(k)])
+                dr, dc, variations[i, k] = dual_update(
+                    e[i][k], e[i][(k + 1) % 3], e[(i + 1) % (blocks + 1)][k], dr, dc, no_row=no_row, no_col=no_cols[k]
+                )
+                side_r[i, :, at(k)] = dr
+                side_c[i, :, at(k)] = dc
+        for i in range(blocks + 1):
+            for k in range(3):
+                t = cols_of[k]
+                p = img[i, :, at(t)] if step == 0 else side_prim[i, :, at(k)]
+                updated = primal_update(
+                    p, side_r[i, :, at(k)], side_c[i, :, at(k)], side_r[(i + blocks) % (blocks + 1), :, at(k)],
+                    side_c[i, :, at((k + 2) % 3)], gain[i, :, at(t)], bias[i, :, at(t)],
+                )
+                if step < ITERS - 1:
+                    side_ext[i, :, at(k)] = 2.0 * updated - p
+                side_prim[i, :, at(k)] = updated
+                if k != 1 and i < blocks:
+                    term = loss(variations[i, k], fid[i, :, at(t)], updated - img[i, :, at(t)])
+                    partial = partial + jnp.where(lane < TW // 2 if k == 2 else lane >= TW // 2, term, 0.0)
+        acc[step] = partial
+
+    for t in range(1, last_t):
+        staged[2 * t, 0] = strip_prim[2, :HALF, at(t)]
+        staged[2 * t + 1, last] = strip_prim[0, HALF:, at(t)]
+    for k, t in ((2, 0), (0, last_t)):
+        for i in range(blocks):
+            value = prim[i, :, at(t)]
+            if i == 0:
+                value = jnp.where(sub < HALF, strip_prim[2, :, at(t)], value)
+            if i == last:
+                value = jnp.where(sub >= HALF, strip_prim[0, :, at(t)], value)
+            value = jnp.where(lane < TW // 2 if k == 2 else lane >= TW // 2, side_prim[i, :, at(k)], value)
+            staged[2 * t, i] = value[:HALF]
+            staged[2 * t + 1, i] = value[HALF:]
 
     lane_1 = lax.broadcasted_iota(jnp.int32, (1, TW), 1)
     sums = jnp.zeros((1, TW), jnp.float32)
@@ -203,20 +331,6 @@
     part_src[...] = sums
     part_rows[r] = sums
 
-    @pl.loop(0, blocks)
-    def _(i):
-        p = prim[i]
-        for t in range(tiles):
-            tile = p[:, t * TW : (t + 1) * TW]
-            staged[2 * t, i] = tile[:HALF]
-            staged[2 * t + 1, i] = tile[HALF:]
-
-    def spread_to(m):
-        return pltpu.make_async_remote_copy(
-            src_ref=staged.at[m], dst_ref=spread.at[r], send_sem=send1, recv_sem=recv1,
-            device_id=(m, c), device_id_type=MESH,
-        )
-
     def part_to(m):
         return pltpu.make_async_remote_copy(
             src_ref=part_src, dst_ref=part_rows.at[r], send_sem=psend, recv_sem=precv,
@@ -225,7 +339,16 @@
 
     @pl.loop(1, n_rows)
     def _(j):
-        spread_to(lax.rem(r + j, n_rows)).start()
+        m = lax.rem(r + j, n_rows)
+        inner = (m >= 2) & (m < n_rows - 2)
+
+        @pl.when(inner)
+        def _():
+            spread_to(m, last * lax.rem(m, 2), 1).start()
+
+        @pl.when(jnp.logical_not(inner))
+        def _():
+            spread_to(m, 0, blocks).start()
 
     @pl.loop(1, n_rows)
     def _(j):
@@ -327,7 +450,10 @@
     pieces = pltpu.VMEM((n_rows, blocks, HALF, TW), f32)
     dma = pltpu.SemaphoreType.DMA
     scratch = (
-        [ringed] * 8
+        [ringed] * 4
+        + [pltpu.VMEM((blocks, BR, width), f32)] * 4
+        + [pltpu.VMEM((3, BR, width), f32)] * 4
+        + [pltpu.VMEM((blocks + 1, BR, 3 * TW), f32)] * 4
         + [
             pltpu.VMEM((blocks, BR, width), jnp.int32),
             pltpu.VMEM((2, BR, width), f32),

time: 55.7 us -> 62.7 us (1.13)
  Pallas kernels: 52.5 us -> 59.5 us
    pallas_call x1, Pallas kernels: 52.5 us -> 59.5 us  [per_device(): pl.pallas_call(functools.partial(kernel, n_rows, n_cols, blocks, tiles, p...]
where the time goes in v2:
time: 62.7 us; the launch traced here: 62.6 us
  Pallas kernels  59.5 us (95%)
  local copies, waits for them, and re-layouts  2.39 us (4%)
  between operations  0.65 us (1%)
    pallas_call x1, Pallas kernels, per_device(): pl.pallas_call(functools.partial(kernel, n_rows, n_cols, blocks, tiles, p...  59.5 us
    unnamed x4, local copies, waits for them, and re-layouts  2.39 us

profile of v2, /device:TPU:1, one launch (start us, length us, event | category | flops | bytes accessed | tf_op | source)
XLA Modules:
  0.0 62.6 jit_solution(1965526748431837228)
XLA Ops:
  0.6 59.5 %shard_map.59 = (f32[8,8,2048]{2,1,0:T(8,128)}, f32[3]{0:T(128)}) custom-call(f32[8,8,2048]{2,1,0:T(8,128)} %bitcast.4, s32[8,8,2048]{2,1,0:T(8,128)} %bitcast.5, s32[8,16]{1,0:T(8,128)} %weight_ref.1, s32[1,256]{1,0:T(1,128)} %bitcast.7), custom_call_target="tpu_custom_call" | custom-call | tf_op jit(solution)/shard_map/pallas_call | solution.py:480
  60.2 0.0 copy-start
  60.2 1.9 %copy.8 = f32[64,2048]{1,0:T(8,128)} copy(f32[64,2048]{1,0:T(8,128)} %bitcast.6) | data formatting | bytes 1048576
  62.0 0.0 copy-done
  62.0 0.5 copy.9
Async XLA Ops:
  60.2 1.9 %copy-start = (f32[3]{0:T(128)S(1)}, f32[3]{0:T(128)}, u32[]{:S(2)}) copy-start(f32[3]{0:T(128)} %get-tuple-element.9) | copy-start | bytes 40

commit v3 on v2

--- a/solution.py
+++ b/solution.py
@@ -95,6 +95,11 @@
             weight = weight_ref[i, t].astype(jnp.float32) * fidelity_scale
             fid[i, :, at(t)] = weight * (1 - mask_v[i, :, at(t)]).astype(jnp.float32)
             coefficients(i, at(t))
+            value = img[i, :, at(t)]
+            prim[i, :, at(t)] = value
+            ext[i, :, at(t)] = value
+            dual_r[i, :, at(t)] = jnp.zeros((BR, TW), jnp.float32)
+            dual_c[i, :, at(t)] = jnp.zeros((BR, TW), jnp.float32)
 
     row_msg[0] = jnp.where(sub_w < HALF, img[0, :, pl.ds(0, width)], pltpu.roll(fid[0, :, pl.ds(0, width)], HALF, 0))
     row_msg[1] = jnp.where(
@@ -118,10 +123,7 @@
             grad_r = jnp.where(sub == no_row, 0.0, grad_r)
         if no_col is not None:
             grad_c = jnp.where(lane == no_col, 0.0, grad_c)
-        trial_r = sigma_step * grad_r
-        trial_c = sigma_step * grad_c
-        if dr is not None:
-            trial_r, trial_c = dr + trial_r, dc + trial_c
+        trial_r, trial_c = dr + sigma_step * grad_r, dc + sigma_step * grad_c
         scale = jnp.minimum(1.0, tv_weight * lax.rsqrt(trial_r * trial_r + trial_c * trial_c))
         return trial_r * scale, trial_c * scale, jnp.sqrt(grad_r * grad_r + grad_c * grad_c)
 
@@ -133,44 +135,40 @@
     def loss(variation, f, misfit):
         return tv_weight * variation + 0.5 * f * (misfit * misfit)
 
-    for step in range(ITERS):
-        old = img if step == 0 else ext
-        old_prim = img if step == 0 else prim
-
-        def body(i, partial, step=step, old=old, old_prim=old_prim):
-            following, previous = jnp.minimum(i + 1, last), jnp.maximum(i - 1, 0)
-            row = jnp.zeros((BR, TW), jnp.float32)
-            e = old[i, :, at(0)]
-            dc_left = None
+    zero = jnp.zeros((BR, TW), jnp.float32)
+
+    @pl.loop(0, ITERS)
+    def _(step):
+        partial = [zero, zero]
+        for i in range(blocks):
             for t in range(tiles):
-                e_right = old[i, :, at(min(t + 1, last_t))]
-                dr, dc = (None, None) if step == 0 else (dual_r[i, :, at(t)], dual_c[i, :, at(t)])
-                dr, dc, variation = dual_update(e, e_right, old[following, :, at(t)], dr, dc)
+                e = ext[i, :, at(t)]
+                dr, dc, variation = dual_update(
+                    e, ext[i, :, at(min(t + 1, last_t))], ext[min(i + 1, last), :, at(t)],
+                    dual_r[i, :, at(t)], dual_c[i, :, at(t)],
+                )
                 dual_r[i, :, at(t)] = dr
                 dual_c[i, :, at(t)] = dc
-                p = old_prim[i, :, at(t)]
+                p = prim[i, :, at(t)]
                 updated = primal_update(
-                    p, dr, dc, dual_r[previous, :, at(t)], dc if t == 0 else dc_left, gain[i, :, at(t)], bias[i, :, at(t)]
-                )
-                dc_left = dc
-                if step < ITERS - 1:
-                    ext[i, :, at(t)] = 2.0 * updated - p
-                else:
-                    staged[2 * t, i] = updated[:HALF]
-                    staged[2 * t + 1, i] = updated[HALF:]
+                    p, dr, dc, dual_r[max(i - 1, 0), :, at(t)], dual_c[i, :, at(max(t - 1, 0))],
+                    gain[i, :, at(t)], bias[i, :, at(t)],
+                )
+                ext[i, :, at(t)] = 2.0 * updated - p
                 prim[i, :, at(t)] = updated
                 term = loss(variation, fid[i, :, at(t)], updated - img[i, :, at(t)])
-                if t == 0:
-                    term = jnp.where(lane >= TW // 2, term, 0.0)
-                if t == last_t:
-                    term = jnp.where(lane < TW // 2, term, 0.0)
-                row = row + term
-                e = e_right
-            first = jnp.where(i == 0, HALF, 0)
-            end = jnp.where(i == last, HALF, BR)
-            return partial + jnp.where((sub >= first) & (sub < end), row, 0.0)
-
-        acc[step] = lax.fori_loop(0, blocks, body, jnp.zeros((BR, TW), jnp.float32))
+                if i in (0, last):
+                    term = jnp.where(sub >= HALF if i == 0 else sub < HALF, term, 0.0)
+                if t in (0, last_t):
+                    term = jnp.where(lane >= TW // 2 if t == 0 else lane < TW // 2, term, 0.0)
+                partial[t % 2] = partial[t % 2] + term
+        acc[step] = partial[0] + partial[1]
+
+    for i in range(blocks):
+        for t in range(tiles):
+            value = prim[i, :, at(t)]
+            staged[2 * t, i] = value[:HALF]
+            staged[2 * t + 1, i] = value[HALF:]
 
     pl.semaphore_wait(barrier, n_rows - 1 + n_cols - 1 + 4)
 
@@ -228,81 +226,76 @@
     for i in range(blocks):
         coefficients(i, at(tiles))
 
-    zero = jnp.zeros((BR, TW), jnp.float32)
-
-    rows_of = (last, blocks, 0)
+    rows_of, cols_of = (last, blocks, 0), (last_t, tiles, 0)
     no_rows = (jnp.where(r == n_rows - 1, BR - 1, BR), jnp.where(r == 0, BR - 1, BR), None)
-    group = 4
-
-    for step in range(ITERS):
-
-        def strip_body(q, partial, step=step):
-            def source(refs, k, t):
-                return img[rows_of[k], :, at(t)] if step == 0 else refs[k, :, at(t)]
-
-            for n in range(group):
-                t = q * group + n
-                before, after = jnp.maximum(t - 1, 0), jnp.minimum(t + 1, last_t)
-                e = [source(strip_ext, k, t) for k in range(3)]
-                duals = []
-                for k in range(3):
-                    dr, dc = (None, None) if step == 0 else (strip_r[k, :, at(t)], strip_c[k, :, at(t)])
-                    duals.append(
-                        dual_update(e[k], source(strip_ext, k, after), e[(k + 1) % 3], dr, dc, no_row=no_rows[k])
+    no_cols = (jnp.where(c == n_cols - 1, TW - 1, TW), jnp.where(c == 0, TW - 1, TW), None)
+
+    for k in range(3):
+        for t in range(tiles):
+            value = img[rows_of[k], :, at(t)]
+            strip_prim[k, :, at(t)] = value
+            strip_ext[k, :, at(t)] = value
+            strip_r[k, :, at(t)] = zero
+            strip_c[k, :, at(t)] = zero
+    for i in range(blocks + 1):
+        for k in range(3):
+            value = img[i, :, at(cols_of[k])]
+            side_prim[i, :, at(k)] = value
+            side_ext[i, :, at(k)] = value
+            side_r[i, :, at(k)] = zero
+            side_c[i, :, at(k)] = zero
+
+    @pl.loop(0, ITERS)
+    def _(step):
+        partial = acc[step]
+        for t in range(tiles):
+            e = [strip_ext[k, :, at(t)] for k in range(3)]
+            duals = []
+            for k in range(3):
+                duals.append(
+                    dual_update(
+                        e[k], strip_ext[k, :, at(min(t + 1, last_t))], e[(k + 1) % 3],
+                        strip_r[k, :, at(t)], strip_c[k, :, at(t)], no_row=no_rows[k],
                     )
-                for k in range(3):
-                    dr, dc, variation = duals[k]
-                    dc_left = strip_c[k, :, at(before)] if n or step else jnp.where(q == 0, dc, strip_c[k, :, at(before)])
-                    strip_r[k, :, at(t)] = dr
-                    strip_c[k, :, at(t)] = dc
-                    p = source(strip_prim, k, t)
-                    i = rows_of[k]
-                    updated = primal_update(
-                        p, dr, dc, duals[(k + 2) % 3][0], dc_left, gain[i, :, at(t)], bias[i, :, at(t)]
-                    )
-                    if step < ITERS - 1:
-                        strip_ext[k, :, at(t)] = 2.0 * updated - p
-                    strip_prim[k, :, at(t)] = updated
-                    if k != 1:
-                        term = loss(variation, fid[i, :, at(t)], updated - img[i, :, at(t)])
-                        keep = sub < HALF if k == 2 else sub >= HALF
-                        if n == 0:
-                            keep = keep & (lane >= jnp.where(q == 0, TW // 2, 0))
-                        if n == group - 1:
-                            keep = keep & (lane < jnp.where(t == last_t, TW // 2, TW))
-                        partial = partial + jnp.where(keep, term, 0.0)
-            return partial
-
-        acc[step] = lax.fori_loop(0, tiles // group, strip_body, acc[step])
-
-    cols_of = (last_t, tiles, 0)
-    no_cols = (jnp.where(c == n_cols - 1, TW - 1, TW), jnp.where(c == 0, TW - 1, TW), None)
-    for step in range(ITERS):
-        partial = acc[step]
-        e = [
-            [img[i, :, at(cols_of[k])] if step == 0 else side_ext[i, :, at(k)] for k in range(3)]
-            for i in range(blocks + 1)
-        ]
+                )
+            for k in range(3):
+                dr, dc, variation = duals[k]
+                strip_r[k, :, at(t)] = dr
+                strip_c[k, :, at(t)] = dc
+                p = strip_prim[k, :, at(t)]
+                i = rows_of[k]
+                updated = primal_update(
+                    p, dr, dc, duals[(k + 2) % 3][0], strip_c[k, :, at(max(t - 1, 0))],
+                    gain[i, :, at(t)], bias[i, :, at(t)],
+                )
+                strip_ext[k, :, at(t)] = 2.0 * updated - p
+                strip_prim[k, :, at(t)] = updated
+                if k != 1:
+                    term = loss(variation, fid[i, :, at(t)], updated - img[i, :, at(t)])
+                    term = jnp.where(sub < HALF if k == 2 else sub >= HALF, term, 0.0)
+                    if t in (0, last_t):
+                        term = jnp.where(lane >= TW // 2 if t == 0 else lane < TW // 2, term, 0.0)
+                    partial = partial + term
         variations = {}
+        e = [[side_ext[i, :, at(k)] for k in range(3)] for i in range(blocks + 1)]
         for i in range(blocks + 1):
             no_row = no_rows[0] if i == last else no_rows[1] if i == blocks else None
             for k in range(3):
-                dr, dc = (None, None) if step == 0 else (side_r[i, :, at(k)], side_c[i, :, at(k)])
                 dr, dc, variations[i, k] = dual_update(
-                    e[i][k], e[i][(k + 1) % 3], e[(i + 1) % (blocks + 1)][k], dr, dc, no_row=no_row, no_col=no_cols[k]
+                    e[i][k], e[i][(k + 1) % 3], e[(i + 1) % (blocks + 1)][k],
+                    side_r[i, :, at(k)], side_c[i, :, at(k)], no_row=no_row, no_col=no_cols[k],
                 )
                 side_r[i, :, at(k)] = dr
                 side_c[i, :, at(k)] = dc
         for i in range(blocks + 1):
             for k in range(3):
                 t = cols_of[k]
-                p = img[i, :, at(t)] if step == 0 else side_prim[i, :, at(k)]
+                p = side_prim[i, :, at(k)]
                 updated = primal_update(
                     p, side_r[i, :, at(k)], side_c[i, :, at(k)], side_r[(i + blocks) % (blocks + 1), :, at(k)],
                     side_c[i, :, at((k + 2) % 3)], gain[i, :, at(t)], bias[i, :, at(t)],
                 )
-                if step < ITERS - 1:
-                    side_ext[i, :, at(k)] = 2.0 * updated - p
+                side_ext[i, :, at(k)] = 2.0 * updated - p
                 side_prim[i, :, at(k)] = updated
                 if k != 1 and i < blocks:
                     term = loss(variations[i, k], fid[i, :, at(t)], updated - img[i, :, at(t)])

time: 62.7 us -> 48.3 us (0.77)
  Pallas kernels: 59.5 us -> 45.1 us
    pallas_call x1, Pallas kernels: 59.5 us -> 45.1 us  [per_device(): pl.pallas_call(functools.partial(kernel, n_rows, n_cols, blocks, tiles, p...]
where the time goes in v3:
time: 48.3 us; the launch traced here: 48.1 us
  Pallas kernels  45.1 us (93%)
  local copies, waits for them, and re-layouts  2.39 us (5%)
  between operations  0.65 us (1%)
    pallas_call x1, Pallas kernels, per_device(): pl.pallas_call(functools.partial(kernel, n_rows, n_cols, blocks, tiles, p...  45.1 us
    unnamed x4, local copies, waits for them, and re-layouts  2.39 us

profile of v3, /device:TPU:1, one launch (start us, length us, event | category | flops | bytes accessed | tf_op | source)
XLA Modules:
  0.0 48.1 jit_solution(12757326612772952780)
XLA Ops:
  0.6 45.1 %shard_map.59 = (f32[8,8,2048]{2,1,0:T(8,128)}, f32[3]{0:T(128)}) custom-call(f32[8,8,2048]{2,1,0:T(8,128)} %bitcast.4, s32[8,8,2048]{2,1,0:T(8,128)} %bitcast.5, s32[8,16]{1,0:T(8,128)} %weight_ref.1, s32[1,256]{1,0:T(1,128)} %bitcast.7), custom_call_target="tpu_custom_call" | custom-call | tf_op jit(solution)/shard_map/pallas_call | solution.py:473
  45.7 0.0 copy-start
  45.7 1.9 %copy.8 = f32[64,2048]{1,0:T(8,128)} copy(f32[64,2048]{1,0:T(8,128)} %bitcast.6) | data formatting | bytes 1048576
  47.6 0.0 copy-done
  47.6 0.5 %copy.9 = f32[3]{0:T(128)} copy(f32[3]{0:T(128)S(1)} %copy-done) | data formatting | bytes 24
Async XLA Ops:
  45.7 1.9 %copy-start = (f32[3]{0:T(128)S(1)}, f32[3]{0:T(128)}, u32[]{:S(2)}) copy-start(f32[3]{0:T(128)} %get-tuple-element.9) | copy-start | bytes 40

commit v4 on v3

--- a/solution.py
+++ b/solution.py
@@ -23,14 +23,14 @@
 def kernel(
     n_rows, n_cols, blocks, tiles, pixel_total,
     image_hbm, mask_hbm, weight_ref, owner_ref,
-    out_hbm, objective_ref,
+    gathered, objective_ref,
     img, fid, gain, bias, prim, ext, dual_r, dual_c,
     strip_prim, strip_ext, strip_r, strip_c, side_prim, side_ext, side_r, side_c, mask_v,
     row_msg, row_got, col_msg, col_got, corner_got,
-    staged, spread, sorted_, gathered, out_v,
+    staged, spread, sorted_,
     order_v, order_s, acc, part_src, part_rows, part_src_c, part_cols,
     load_sem, order_sem, halo_send, halo_recv,
-    send1, recv1, send2, recv2, psend, precv, csend, crecv, out_sem,
+    send1, recv1, send2, recv2, psend, precv, csend, crecv, ready,
 ):
     width = tiles * TW
     ring = width + TW
@@ -44,22 +44,41 @@
     load_image.start()
     load_mask.start()
 
+    span = 4
+    depth = n_rows // span
+
+    def peer(j):
+        near = lax.rem(lax.rem(r, depth) + lax.div(j, span), depth)
+        return lax.rem(lax.div(r, depth) + lax.rem(j, span), span) * depth + near
+
     barrier = pltpu.get_barrier_semaphore()
+    odd = lax.rem(c, 2) == 1
+    even = jnp.logical_not(odd)
+    opposite = n_cols // 2
+
+    def across(signal):
+        for n in range(opposite):
+            signal(r, lax.rem(c + 2 * n + 1, n_cols))
+        for row in (up, down):
+            for col in (left, right):
+                signal(row, col)
 
     def greet(row, col):
         pl.semaphore_signal(barrier, inc=1, device_id=(row, col), device_id_type=MESH)
 
-    @pl.loop(1, n_cols)
-    def _(j):
-        greet(r, lax.rem(c + j, n_cols))
-
-    for row in (up, down):
-        for col in (left, right):
-            greet(row, col)
+    def answer(row, col):
+        pl.semaphore_signal(ready, inc=1, device_id=(row, col), device_id_type=MESH)
+
+    @pl.when(even)
+    def _():
+        across(greet)
+
+    for n in range(1, opposite):
+        greet(r, lax.rem(c + 2 * n, n_cols))
 
     @pl.loop(1, n_rows)
     def _(j):
-        greet(lax.rem(r + j, n_rows), c)
+        greet(peer(j), c)
 
     total = n_rows * blocks
     own = jnp.broadcast_to(owner_ref[...], (total, total))
@@ -115,6 +134,32 @@
             axis=0,
         ).T
         col_msg[side] = both[:BR] if side == 0 else both[TW - BR :]
+
+    first_tile, last_tile = pl.ds(0, TW), pl.ds(width - TW, TW)
+    messages = (
+        (row_msg.at[0], row_got.at[0], up, c),
+        (row_msg.at[1], row_got.at[1], down, c),
+        (col_msg.at[0], col_got.at[0], r, left),
+        (col_msg.at[1], col_got.at[1], r, right),
+        (row_msg.at[0, :, first_tile], corner_got.at[0], up, left),
+        (row_msg.at[0, :, last_tile], corner_got.at[1], up, right),
+        (row_msg.at[1, :, first_tile], corner_got.at[2], down, left),
+        (row_msg.at[1, :, last_tile], corner_got.at[3], down, right),
+    )
+    halos = [
+        pltpu.make_async_remote_copy(
+            src_ref=src, dst_ref=dst, send_sem=halo_send.at[k], recv_sem=halo_recv.at[k],
+            device_id=(row, col), device_id_type=MESH,
+        )
+        for k, (src, dst, row, col) in enumerate(messages)
+    ]
+
+    @pl.when(odd)
+    def _():
+        pl.semaphore_wait(barrier, n_rows - 1 + n_cols - 1 + 4)
+        across(answer)
+        for halo in halos[2:] + halos[:2]:
+            halo.start()
 
     def dual_update(e, e_right, e_below, dr, dc, no_row=None, no_col=None):
         grad_r = pltpu.roll(jnp.where(sub == 0, e_below, e), BR - 1, 0) - e
@@ -170,29 +215,6 @@
             staged[2 * t, i] = value[:HALF]
             staged[2 * t + 1, i] = value[HALF:]
 
-    pl.semaphore_wait(barrier, n_rows - 1 + n_cols - 1 + 4)
-
-    first_tile, last_tile = pl.ds(0, TW), pl.ds(width - TW, TW)
-    messages = (
-        (row_msg.at[0], row_got.at[0], up, c),
-        (row_msg.at[1], row_got.at[1], down, c),
-        (col_msg.at[0], col_got.at[0], r, left),
-        (col_msg.at[1], col_got.at[1], r, right),
-        (row_msg.at[0, :, first_tile], corner_got.at[0], up, left),
-        (row_msg.at[0, :, last_tile], corner_got.at[1], up, right),
-        (row_msg.at[1, :, first_tile], corner_got.at[2], down, left),
-        (row_msg.at[1, :, last_tile], corner_got.at[3], down, right),
-    )
-    halos = [
-        pltpu.make_async_remote_copy(
-            src_ref=src, dst_ref=dst, send_sem=halo_send.at[k], recv_sem=halo_recv.at[k],
-            device_id=(row, col), device_id_type=MESH,
-        )
-        for k, (src, dst, row, col) in enumerate(messages)
-    ]
-    for k in (2, 3, 4, 5, 6, 7, 0, 1):
-        halos[k].start()
-
     def spread_to(m, start, size):
         piece = pl.ds(start, size)
         return pltpu.make_async_remote_copy(
@@ -200,13 +222,25 @@
             device_id=(m, c), device_id_type=MESH,
         )
 
+    @pl.when(even)
+    def _():
+        pl.semaphore_wait(barrier, n_rows - 1 + opposite - 1)
+        for halo in halos[:2]:
+            halo.start()
+
     @pl.loop(1, n_rows)
     def _(j):
-        m = lax.rem(r + j, n_rows)
+        m = peer(j)
 
         @pl.when((m >= 2) & (m < n_rows - 2))
         def _():
             spread_to(m, 1 - lax.rem(m, 2), last).start()
+
+    @pl.when(even)
+    def _():
+        pl.semaphore_wait(ready, opposite + 4)
+        for halo in halos[2:]:
+            halo.start()
 
     for halo in halos:
         halo.wait_recv()
@@ -332,7 +366,11 @@
 
     @pl.loop(1, n_rows)
     def _(j):
-        m = lax.rem(r + j, n_rows)
+        part_to(peer(j)).start()
+
+    @pl.loop(1, n_rows)
+    def _(j):
+        m = peer(j)
         inner = (m >= 2) & (m < n_rows - 2)
 
         @pl.when(inner)
@@ -342,10 +380,6 @@
         @pl.when(jnp.logical_not(inner))
         def _():
             spread_to(m, 0, blocks).start()
-
-    @pl.loop(1, n_rows)
-    def _(j):
-        part_to(lax.rem(r + j, n_rows)).start()
 
     spread[r] = staged[r]
     to_scalars.wait()
@@ -356,28 +390,6 @@
     )
     all_spread.wait_recv()
 
-    def collect_to(d):
-        return pltpu.make_async_remote_copy(
-            src_ref=sorted_.at[d], dst_ref=gathered.at[r], send_sem=send2, recv_sem=recv2,
-            device_id=(d, c), device_id_type=MESH,
-        )
-
-    def sort_for(d):
-        for k in range(blocks):
-            b = order_s[0, d * blocks + k]
-            sorted_[d, k] = spread[b // blocks, lax.rem(b, blocks)]
-
-    sort_for(lax.rem(r + 1, n_rows))
-
-    @pl.loop(2, n_rows)
-    def _(j):
-        sort_for(lax.rem(r + j, n_rows))
-        collect_to(lax.rem(r + j - 1, n_rows)).start()
-
-    sort_for(r)
-    collect_to(up).start()
-    gathered[r] = sorted_[r]
-
     all_parts = pltpu.make_async_remote_copy(
         src_ref=part_rows.at[peers], dst_ref=part_rows.at[peers], send_sem=psend, recv_sem=precv,
         device_id=(up, c), device_id_type=MESH,
@@ -399,6 +411,28 @@
     def _(j):
         part_across(lax.rem(c + j, n_cols)).start()
 
+    def collect_to(d):
+        return pltpu.make_async_remote_copy(
+            src_ref=sorted_.at[d], dst_ref=gathered.at[r], send_sem=send2, recv_sem=recv2,
+            device_id=(d, c), device_id_type=MESH,
+        )
+
+    def sort_for(d):
+        for k in range(blocks):
+            b = order_s[0, d * blocks + k]
+            sorted_[d, k] = spread[b // blocks, lax.rem(b, blocks)]
+
+    sort_for(peer(1))
+
+    @pl.loop(2, n_rows)
+    def _(j):
+        sort_for(peer(j))
+        collect_to(peer(j - 1)).start()
+
+    sort_for(r)
+    collect_to(peer(n_rows - 1)).start()
+    gathered[r] = sorted_[r]
+
     col_peers = pl.ds(0, n_cols - 1)
     all_cols = pltpu.make_async_remote_copy(
         src_ref=part_cols.at[col_peers], dst_ref=part_cols.at[col_peers], send_sem=csend, recv_sem=crecv,
@@ -408,8 +442,7 @@
     everywhere = part_cols[0]
     for s in range(1, n_cols):
         everywhere = everywhere + part_cols[s]
-    for step in range(ITERS):
-        objective_ref[step] = jnp.sum(jnp.where(lane_1 == step, everywhere, 0.0)) / pixel_total
+    objective_ref[...] = everywhere / pixel_total
 
     all_collected = pltpu.make_async_remote_copy(
         src_ref=sorted_.at[peers], dst_ref=gathered.at[peers], send_sem=send2, recv_sem=recv2,
@@ -417,20 +450,26 @@
     )
     all_collected.wait_recv()
 
-    @pl.loop(0, blocks)
-    def _(k):
-        for t in range(tiles):
-            out_v[k, :, pl.ds(t * TW, TW)] = jnp.concatenate([gathered[2 * t, k], gathered[2 * t + 1, k]], axis=0)
-
-    store = pltpu.make_async_copy(out_v, out_hbm, out_sem)
-    store.start()
     for halo in halos:
         halo.wait_send()
     all_spread.wait_send()
     all_parts.wait_send()
     all_cols.wait_send()
     all_collected.wait_send()
-    store.wait()
+
+
+def assemble(pieces, row, out_hbm, objective, out, sems):
+    blocks, _, width = out.shape
+    stores = [pltpu.make_async_copy(out.at[k], out_hbm.at[k], sems.at[k]) for k in range(blocks)]
+    for k in range(blocks):
+        for t in range(width // TW):
+            out[k, :, pl.ds(t * TW, TW)] = jnp.concatenate([pieces[2 * t, k], pieces[2 * t + 1, k]], axis=0)
+        stores[k].start()
+    lanes = lax.broadcasted_iota(jnp.int32, (1, TW), 1)
+    for step in range(ITERS):
+        objective[step] = jnp.sum(jnp.where(lanes == step, row[...], 0.0))
+    for store in stores:
+        store.wait()
 
 
 def per_device(n_rows, n_cols, image, cloud_mask, tile_weight, owner):
@@ -455,9 +494,8 @@
             pltpu.VMEM((2, BR, TW), f32),
             pltpu.VMEM((4, BR, TW), f32),
         ]
-        + [pieces] * 4
+        + [pieces] * 3
         + [
-            pltpu.VMEM((blocks, BR, width), f32),
             pltpu.VMEM((1, n_rows * blocks), jnp.int32),
             pltpu.SMEM((1, n_rows * blocks), jnp.int32),
             pltpu.VMEM((ITERS, BR, TW), f32),
@@ -466,18 +504,19 @@
             pltpu.VMEM((1, TW), f32),
             pltpu.VMEM((n_cols, 1, TW), f32),
             dma((2,)), dma, dma((8,)), dma((8,)),
-            dma, dma, dma, dma, dma, dma, dma, dma, dma,
+            dma, dma, dma, dma, dma, dma, dma, dma,
+            pltpu.SemaphoreType.REGULAR,
         ]
     )
     vmem, smem, hbm = (pl.BlockSpec(memory_space=s) for s in (pltpu.VMEM, pltpu.SMEM, pl.ANY))
-    out, objective = pl.pallas_call(
+    received, row = pl.pallas_call(
         functools.partial(kernel, n_rows, n_cols, blocks, tiles, pixel_total),
         out_shape=(
-            jax.ShapeDtypeStruct((blocks, BR, width), f32),
-            jax.ShapeDtypeStruct((ITERS,), f32),
+            pltpu.VMEM((n_rows, blocks, HALF, TW), f32),
+            pltpu.VMEM((1, TW), f32),
         ),
         in_specs=[hbm, hbm, smem, vmem],
-        out_specs=(hbm, smem),
+        out_specs=(vmem, vmem),
         scratch_shapes=scratch,
         compiler_params=pltpu.CompilerParams(collective_id=0, has_side_effects=True),
     )(
@@ -486,6 +525,13 @@
         tile_weight,
         owner.reshape(1, -1),
     )
+    out, objective = pl.pallas_call(
+        assemble,
+        out_shape=(jax.ShapeDtypeStruct((blocks, BR, width), f32), jax.ShapeDtypeStruct((ITERS,), f32)),
+        in_specs=[vmem, vmem],
+        out_specs=(hbm, smem),
+        scratch_shapes=[pltpu.VMEM((blocks, BR, width), f32), dma((blocks,))],
+    )(pltpu.with_memory_space_constraint(received, pltpu.VMEM), pltpu.with_memory_space_constraint(row, pltpu.VMEM))
     return out.reshape(rows_here, width), objective
 
 

time: 48.3 us -> 44.6 us (0.923)
  the two profiles are of different devices: /device:TPU:1 before, /device:TPU:161 now
where the time goes in v4:
time: 44.6 us; the launch traced here: 44.5 us
  Pallas kernels  43.8 us (98%)
  between operations  0.64 us (1%)
    pallas_call x1, Pallas kernels, per_device(): pl.pallas_call(functools.partial(kernel, n_rows, n_cols, blocks, tiles, p...  42.5 us
    pallas_call x1, Pallas kernels, per_device(): pl.pallas_call(assemble, out_shape=(jax.ShapeDtypeStruct((blocks, BR, wid...  1.38 us

profile of v4, /device:TPU:161, one launch (start us, length us, event | category | flops | bytes accessed | tf_op | source)
XLA Modules:
  0.0 44.5 jit_solution(1602139527692576863)
XLA Ops:
  0.6 42.5 %shard_map.59 = (f32[32,8,4,128]{3,2,1,0:T(4,128)S(1)}, f32[1,128]{1,0:T(1,128)S(1)}) custom-call(f32[8,8,2048]{2,1,0:T(8,128)} %bitcast.4, s32[8,8,2048]{2,1,0:T(8,128)} %bitcast.5, s32[8,16]{1,0:T(8,128)} %weight_ref.1, s32[1,256]{1,0:T(1,128)} %bitcast.6), custom_call_target="tpu_custom_call" | custom-call | tf_op jit(solution)/shard_map/pallas_call | solution.py:512
  43.1 1.4 %shard_map.60 = (f32[8,8,2048]{2,1,0:T(8,128)}, f32[3]{0:T(128)}) custom-call(f32[32,8,4,128]{3,2,1,0:T(4,128)S(1)} %get-tuple-element.6.pieces, f32[1,128]{1,0:T(1,128)S(1)} %get-tuple-element.7.row), custom_call_target="tpu_custom_call" | custom-call | tf_op jit(solution)/shard_map/pallas_call | solution.py:528

commit v5 on v4

--- a/solution.py
+++ b/solution.py
@@ -11,6 +11,7 @@
 TW = 128
 ITERS = 3
 HALF = 4
+PAIR = 2
 
 fidelity_scale = 0.25
 tau_step = 0.35
@@ -23,15 +24,16 @@
 def kernel(
     n_rows, n_cols, blocks, tiles, pixel_total,
     image_hbm, mask_hbm, weight_ref, owner_ref,
-    gathered, objective_ref,
+    gathered, edge_gathered, objective_ref,
     img, fid, gain, bias, prim, ext, dual_r, dual_c,
     strip_prim, strip_ext, strip_r, strip_c, side_prim, side_ext, side_r, side_c, mask_v,
     row_msg, row_got, col_msg, col_got, corner_got,
-    staged, spread, sorted_,
+    staged, spread_0, spread_1, sorted_, edge_staged, edge_spread, edge_sorted,
     order_v, order_s, acc, part_src, part_rows, part_src_c, part_cols,
     load_sem, order_sem, halo_send, halo_recv,
-    send1, recv1, send2, recv2, psend, precv, csend, crecv, ready,
+    send1, recv1, send2, recv2, psend, precv, csend, crecv, esend1, erecv1, esend2, erecv2, ready,
 ):
+    spread = (spread_0, spread_1)
     width = tiles * TW
     ring = width + TW
     r = lax.axis_index("rows")
@@ -98,6 +100,10 @@
     lane = lax.broadcasted_iota(jnp.int32, (BR, TW), 1)
     sub_w = lax.broadcasted_iota(jnp.int32, (BR, width), 0)
     last, last_t = blocks - 1, tiles - 1
+
+    def stage(block, m, value):
+        for q in range(2):
+            staged[q, m, block] = value[q * PAIR : (q + 1) * PAIR]
 
     def at(t):
         return pl.ds(t * TW if isinstance(t, int) else pl.multiple_of(t * TW, TW), TW)
@@ -210,15 +216,15 @@
         acc[step] = partial[0] + partial[1]
 
     for i in range(blocks):
-        for t in range(tiles):
+        for t in range(1, last_t):
             value = prim[i, :, at(t)]
-            staged[2 * t, i] = value[:HALF]
-            staged[2 * t + 1, i] = value[HALF:]
-
-    def spread_to(m, start, size):
+            stage(i, 2 * t, value[:HALF])
+            stage(i, 2 * t + 1, value[HALF:])
+
+    def spread_to(q, m, start, size):
         piece = pl.ds(start, size)
         return pltpu.make_async_remote_copy(
-            src_ref=staged.at[m, piece], dst_ref=spread.at[r, piece], send_sem=send1, recv_sem=recv1,
+            src_ref=staged.at[q, m, piece], dst_ref=spread[q].at[r, piece], send_sem=send1.at[q], recv_sem=recv1.at[q],
             device_id=(m, c), device_id_type=MESH,
         )
 
@@ -234,31 +240,15 @@
 
         @pl.when((m >= 2) & (m < n_rows - 2))
         def _():
-            spread_to(m, 1 - lax.rem(m, 2), last).start()
-
-    @pl.when(even)
-    def _():
-        pl.semaphore_wait(ready, opposite + 4)
-        for halo in halos[2:]:
-            halo.start()
-
-    for halo in halos:
+            spread_to(0, m, 1 - lax.rem(m, 2), last).start()
+
+    for halo in halos[:2]:
         halo.wait_recv()
 
     below, above = row_got[0], row_got[1]
     img[blocks, :, pl.ds(0, width)] = jnp.where(sub_w < HALF, below, above)
     fid[blocks, :, pl.ds(0, width)] = pltpu.roll(jnp.where(sub_w < HALF, above, below), HALF, 0)
-    sides = jnp.concatenate([col_got[0], jnp.zeros((TW - 2 * BR, TW), jnp.float32), col_got[1]], axis=0).T
-    img[pl.ds(0, blocks), :, pl.ds(width, TW)] = sides[:rows_here].reshape(blocks, BR, TW)
-    fid[pl.ds(0, blocks), :, pl.ds(width, TW)] = sides[rows_here:].reshape(blocks, BR, TW)
-    low = jnp.where(lane < TW // 2, corner_got[0], corner_got[1])
-    high = jnp.where(lane < TW // 2, corner_got[2], corner_got[3])
-    img[blocks, :, pl.ds(width, TW)] = jnp.where(sub < HALF, low, high)
-    fid[blocks, :, pl.ds(width, TW)] = pltpu.roll(jnp.where(sub < HALF, high, low), HALF, 0)
-
-    coefficients(blocks, pl.ds(0, ring))
-    for i in range(blocks):
-        coefficients(i, at(tiles))
+    coefficients(blocks, pl.ds(0, width))
 
     rows_of, cols_of = (last, blocks, 0), (last_t, tiles, 0)
     no_rows = (jnp.where(r == n_rows - 1, BR - 1, BR), jnp.where(r == 0, BR - 1, BR), None)
@@ -271,13 +261,6 @@
             strip_ext[k, :, at(t)] = value
             strip_r[k, :, at(t)] = zero
             strip_c[k, :, at(t)] = zero
-    for i in range(blocks + 1):
-        for k in range(3):
-            value = img[i, :, at(cols_of[k])]
-            side_prim[i, :, at(k)] = value
-            side_ext[i, :, at(k)] = value
-            side_r[i, :, at(k)] = zero
-            side_c[i, :, at(k)] = zero
 
     @pl.loop(0, ITERS)
     def _(step):
@@ -310,6 +293,121 @@
                     if t in (0, last_t):
                         term = jnp.where(lane >= TW // 2 if t == 0 else lane < TW // 2, term, 0.0)
                     partial = partial + term
+        acc[step] = partial
+
+    for t in range(1, last_t):
+        stage(0, 2 * t, strip_prim[2, :HALF, at(t)])
+        stage(last, 2 * t + 1, strip_prim[0, HALF:, at(t)])
+
+    @pl.loop(1, n_rows)
+    def _(j):
+        m = peer(j)
+
+        @pl.when((m >= 2) & (m < n_rows - 2))
+        def _():
+            spread_to(0, m, last * lax.rem(m, 2), 1).start()
+
+    @pl.when(even)
+    def _():
+        pl.semaphore_wait(ready, opposite + 4)
+        for halo in halos[2:]:
+            halo.start()
+
+    @pl.loop(1, n_rows)
+    def _(j):
+        m = peer(j)
+
+        @pl.when((m >= 2) & (m < n_rows - 2))
+        def _():
+            spread_to(1, m, 0, blocks).start()
+
+    n_edges = 2 * BR
+    inner = (r >= 2) & (r < n_rows - 2)
+    holds_edge = lax.rem(r, 2) == 0
+    no_edge = jnp.logical_not(holds_edge)
+    mine = lax.div(r, 2)
+
+    to_scalars.wait()
+
+    def batch(src, dst, count, send_sem, recv_sem):
+        some = pl.ds(0, count)
+        return pltpu.make_async_remote_copy(
+            src_ref=src.at[some], dst_ref=dst.at[some], send_sem=send_sem, recv_sem=recv_sem,
+            device_id=(up, c), device_id_type=MESH,
+        )
+
+    group = 4
+
+    def targets_of(q):
+        return [peer(q * group + n) for n in range(group)]
+
+    def sort_for(source, target, targets):
+        values = []
+        for d in targets:
+            for k in range(blocks):
+                values.append(source(order_s[0, d * blocks + k]))
+        for n, value in enumerate(values):
+            target(targets[n // blocks], n % blocks, value)
+
+    def sort_and_send(source, target, collect):
+        sort_for(source, target, targets_of(0))
+
+        @pl.loop(1, n_rows // group)
+        def _(q):
+            sort_for(source, target, targets_of(q))
+            for n in range(group):
+                before = (q - 1) * group + n
+
+                @pl.when(before > 0)
+                def _():
+                    collect(peer(before)).start()
+
+        for n in range(group):
+            collect(peer(n_rows - group + n)).start()
+
+    def second_stage(q):
+        def collect_to(d):
+            return pltpu.make_async_remote_copy(
+                src_ref=sorted_.at[q, d], dst_ref=gathered.at[q, r], send_sem=send2.at[q], recv_sem=recv2.at[q],
+                device_id=(d, c), device_id_type=MESH,
+            )
+
+        def source(b):
+            return spread[q][lax.div(b, blocks), lax.rem(b, blocks)]
+
+        def target(d, k, value):
+            sorted_[q, d, k] = value
+
+        @pl.when(inner)
+        def _():
+            spread[q][r] = staged[q, r]
+            batch(staged.at[q], spread[q], n_rows - 1, send1.at[q], recv1.at[q]).wait_recv()
+            sort_and_send(source, target, collect_to)
+            gathered[q, r] = sorted_[q, r]
+
+    for halo in halos[2:]:
+        halo.wait_recv()
+
+    sides = jnp.concatenate([col_got[0], jnp.zeros((TW - 2 * BR, TW), jnp.float32), col_got[1]], axis=0).T
+    img[pl.ds(0, blocks), :, pl.ds(width, TW)] = sides[:rows_here].reshape(blocks, BR, TW)
+    fid[pl.ds(0, blocks), :, pl.ds(width, TW)] = sides[rows_here:].reshape(blocks, BR, TW)
+    low = jnp.where(lane < TW // 2, corner_got[0], corner_got[1])
+    high = jnp.where(lane < TW // 2, corner_got[2], corner_got[3])
+    img[blocks, :, pl.ds(width, TW)] = jnp.where(sub < HALF, low, high)
+    fid[blocks, :, pl.ds(width, TW)] = pltpu.roll(jnp.where(sub < HALF, high, low), HALF, 0)
+    for i in range(blocks + 1):
+        coefficients(i, at(tiles))
+    for i in range(blocks + 1):
+        for k in range(3):
+            value = img[i, :, at(cols_of[k])]
+            side_prim[i, :, at(k)] = value
+            side_ext[i, :, at(k)] = value
+            side_r[i, :, at(k)] = zero
+            side_c[i, :, at(k)] = zero
+
+    @pl.loop(0, ITERS)
+    def _(step):
+        partial = acc[step]
         variations = {}
         e = [[side_ext[i, :, at(k)] for k in range(3)] for i in range(blocks + 1)]
         for i in range(blocks + 1):
@@ -336,10 +434,7 @@
                     partial = partial + jnp.where(lane < TW // 2 if k == 2 else lane >= TW // 2, term, 0.0)
         acc[step] = partial
 
-    for t in range(1, last_t):
-        staged[2 * t, 0] = strip_prim[2, :HALF, at(t)]
-        staged[2 * t + 1, last] = strip_prim[0, HALF:, at(t)]
-    for k, t in ((2, 0), (0, last_t)):
+    for side, k, t in ((0, 2, 0), (1, 0, last_t)):
         for i in range(blocks):
             value = prim[i, :, at(t)]
             if i == 0:
@@ -347,59 +442,16 @@
             if i == last:
                 value = jnp.where(sub >= HALF, strip_prim[0, :, at(t)], value)
             value = jnp.where(lane < TW // 2 if k == 2 else lane >= TW // 2, side_prim[i, :, at(k)], value)
-            staged[2 * t, i] = value[:HALF]
-            staged[2 * t + 1, i] = value[HALF:]
+            for q in range(BR):
+                edge_staged[side * BR + q, i] = value[q : q + 1]
 
     lane_1 = lax.broadcasted_iota(jnp.int32, (1, TW), 1)
     sums = jnp.zeros((1, TW), jnp.float32)
     for step in range(ITERS):
         line = jnp.sum(acc[step], axis=0, keepdims=True)
         sums = jnp.where(lane_1 == step, jnp.sum(line, axis=1, keepdims=True), sums)
-    part_src[...] = sums
-    part_rows[r] = sums
-
-    def part_to(m):
-        return pltpu.make_async_remote_copy(
-            src_ref=part_src, dst_ref=part_rows.at[r], send_sem=psend, recv_sem=precv,
-            device_id=(m, c), device_id_type=MESH,
-        )
-
-    @pl.loop(1, n_rows)
-    def _(j):
-        part_to(peer(j)).start()
-
-    @pl.loop(1, n_rows)
-    def _(j):
-        m = peer(j)
-        inner = (m >= 2) & (m < n_rows - 2)
-
-        @pl.when(inner)
-        def _():
-            spread_to(m, last * lax.rem(m, 2), 1).start()
-
-        @pl.when(jnp.logical_not(inner))
-        def _():
-            spread_to(m, 0, blocks).start()
-
-    spread[r] = staged[r]
-    to_scalars.wait()
-    peers = pl.ds(0, n_rows - 1)
-    all_spread = pltpu.make_async_remote_copy(
-        src_ref=staged.at[peers], dst_ref=spread.at[peers], send_sem=send1, recv_sem=recv1,
-        device_id=(up, c), device_id_type=MESH,
-    )
-    all_spread.wait_recv()
-
-    all_parts = pltpu.make_async_remote_copy(
-        src_ref=part_rows.at[peers], dst_ref=part_rows.at[peers], send_sem=psend, recv_sem=precv,
-        device_id=(up, c), device_id_type=MESH,
-    )
-    all_parts.wait_recv()
-    here = part_rows[0]
-    for s in range(1, n_rows):
-        here = here + part_rows[s]
-    part_src_c[...] = here
-    part_cols[c] = here
+    part_src_c[...] = sums
+    part_cols[c] = sums
 
     def part_across(col):
         return pltpu.make_async_remote_copy(
@@ -411,27 +463,47 @@
     def _(j):
         part_across(lax.rem(c + j, n_cols)).start()
 
-    def collect_to(d):
+    def edge_to(u):
         return pltpu.make_async_remote_copy(
-            src_ref=sorted_.at[d], dst_ref=gathered.at[r], send_sem=send2, recv_sem=recv2,
+            src_ref=edge_staged.at[u], dst_ref=edge_spread.at[pl.ds(r * blocks, blocks)],
+            send_sem=esend1, recv_sem=erecv1, device_id=(2 * u, c), device_id_type=MESH,
+        )
+
+    @pl.loop(0, n_edges)
+    def _(j):
+        u = lax.rem(mine + j, n_edges)
+
+        @pl.when(2 * u != r)
+        def _():
+            edge_to(u).start()
+
+    @pl.when(holds_edge)
+    def _():
+        for i in range(blocks):
+            edge_spread[r * blocks + i] = edge_staged[mine, i]
+
+    second_stage(0)
+    second_stage(1)
+
+    def edge_collect_to(d):
+        return pltpu.make_async_remote_copy(
+            src_ref=edge_sorted.at[d], dst_ref=edge_gathered.at[mine], send_sem=esend2, recv_sem=erecv2,
             device_id=(d, c), device_id_type=MESH,
         )
 
-    def sort_for(d):
-        for k in range(blocks):
-            b = order_s[0, d * blocks + k]
-            sorted_[d, k] = spread[b // blocks, lax.rem(b, blocks)]
-
-    sort_for(peer(1))
-
-    @pl.loop(2, n_rows)
-    def _(j):
-        sort_for(peer(j))
-        collect_to(peer(j - 1)).start()
-
-    sort_for(r)
-    collect_to(peer(n_rows - 1)).start()
-    gathered[r] = sorted_[r]
+    @pl.when(holds_edge)
+    def _():
+        arrived = pl.ds(0, (n_rows - 1) * blocks)
+        pltpu.make_async_remote_copy(
+            src_ref=edge_spread.at[arrived], dst_ref=edge_spread.at[arrived], send_sem=esend1, recv_sem=erecv1,
+            device_id=(up, c), device_id_type=MESH,
+        ).wait_recv()
+
+        def target(d, k, value):
+            edge_sorted[d, k] = value
+
+        sort_and_send(lambda b: edge_spread[b], target, edge_collect_to)
+        edge_gathered[mine] = edge_sorted[r]
 
     col_peers = pl.ds(0, n_cols - 1)
     all_cols = pltpu.make_async_remote_copy(
@@ -439,31 +511,70 @@
         device_id=(r, left), device_id_type=MESH,
     )
     all_cols.wait_recv()
-    everywhere = part_cols[0]
-    for s in range(1, n_cols):
-        everywhere = everywhere + part_cols[s]
+    here = part_cols[0]
+    for n in range(1, n_cols):
+        here = here + part_cols[n]
+    part_src[...] = here
+    part_rows[r] = here
+
+    def part_to(m):
+        return pltpu.make_async_remote_copy(
+            src_ref=part_src, dst_ref=part_rows.at[r], send_sem=psend, recv_sem=precv,
+            device_id=(m, c), device_id_type=MESH,
+        )
+
+    @pl.loop(1, n_rows)
+    def _(j):
+        part_to(peer(j)).start()
+
+    all_parts = batch(part_rows, part_rows, n_rows - 1, psend, precv)
+    all_parts.wait_recv()
+    everywhere = part_rows[0]
+    for n in range(1, n_rows):
+        everywhere = everywhere + part_rows[n]
     objective_ref[...] = everywhere / pixel_total
-
-    all_collected = pltpu.make_async_remote_copy(
-        src_ref=sorted_.at[peers], dst_ref=gathered.at[peers], send_sem=send2, recv_sem=recv2,
-        device_id=(up, c), device_id_type=MESH,
-    )
-    all_collected.wait_recv()
 
     for halo in halos:
         halo.wait_send()
-    all_spread.wait_send()
     all_parts.wait_send()
     all_cols.wait_send()
-    all_collected.wait_send()
-
-
-def assemble(pieces, row, out_hbm, objective, out, sems):
+    pieces = n_rows - 4
+
+    for q in range(2):
+        first = functools.partial(batch, staged.at[q], spread[q], send_sem=send1.at[q], recv_sem=recv1.at[q])
+        second = functools.partial(batch, sorted_.at[q], gathered.at[q], send_sem=send2.at[q], recv_sem=recv2.at[q])
+
+        @pl.when(inner)
+        def _():
+            first(pieces - 1).wait_send()
+            second(n_rows - 1).wait_send()
+            second(pieces - 1).wait_recv()
+
+        @pl.when(jnp.logical_not(inner))
+        def _():
+            first(pieces).wait_send()
+            second(pieces).wait_recv()
+
+    @pl.when(holds_edge)
+    def _():
+        batch(edge_staged, edge_gathered, n_edges - 1, esend1, erecv1).wait_send()
+        batch(edge_sorted, edge_sorted, n_rows - 1, esend2, erecv2).wait_send()
+        batch(edge_gathered, edge_gathered, n_edges - 1, esend2, erecv2).wait_recv()
+
+    @pl.when(no_edge)
+    def _():
+        batch(edge_staged, edge_gathered, n_edges, esend1, erecv1).wait_send()
+        batch(edge_gathered, edge_gathered, n_edges, esend2, erecv2).wait_recv()
+
+
+def assemble(pieces, edges, row, out_hbm, objective, out, sems):
     blocks, _, width = out.shape
     stores = [pltpu.make_async_copy(out.at[k], out_hbm.at[k], sems.at[k]) for k in range(blocks)]
     for k in range(blocks):
-        for t in range(width // TW):
-            out[k, :, pl.ds(t * TW, TW)] = jnp.concatenate([pieces[2 * t, k], pieces[2 * t + 1, k]], axis=0)
+        for t in range(1, width // TW - 1):
+            out[k, :, pl.ds(t * TW, TW)] = jnp.concatenate([pieces[q, 2 * t + h, k] for h in range(2) for q in range(2)], axis=0)
+        for side, start in ((0, 0), (1, width - TW)):
+            out[k, :, pl.ds(start, TW)] = jnp.concatenate([edges[side * BR + q, k] for q in range(BR)], axis=0)
         stores[k].start()
     lanes = lax.broadcasted_iota(jnp.int32, (1, TW), 1)
     for step in range(ITERS):
@@ -479,7 +590,8 @@
     pixel_total = float(n_rows * n_cols * rows_here * width)
     f32 = jnp.float32
     ringed = pltpu.VMEM((blocks + 1, BR, width + TW), f32)
-    pieces = pltpu.VMEM((n_rows, blocks, HALF, TW), f32)
+    half = pltpu.VMEM((n_rows, blocks, PAIR, TW), f32)
+    pieces = pltpu.VMEM((2, n_rows, blocks, PAIR, TW), f32)
     dma = pltpu.SemaphoreType.DMA
     scratch = (
         [ringed] * 4
@@ -494,7 +606,8 @@
             pltpu.VMEM((2, BR, TW), f32),
             pltpu.VMEM((4, BR, TW), f32),
         ]
-        + [pieces] * 3
+        + [pieces, half, half, pieces]
+        + [pltpu.VMEM((n, 1, TW) if n > 99 else (n, blocks, 1, TW), f32) for n in (2 * BR, n_rows * blocks, n_rows)]
         + [
             pltpu.VMEM((1, n_rows * blocks), jnp.int32),
             pltpu.SMEM((1, n_rows * blocks), jnp.int32),
@@ -504,19 +617,20 @@
             pltpu.VMEM((1, TW), f32),
             pltpu.VMEM((n_cols, 1, TW), f32),
             dma((2,)), dma, dma((8,)), dma((8,)),
-            dma, dma, dma, dma, dma, dma, dma, dma,
+            dma((2,)), dma((2,)), dma((2,)), dma((2,)), dma, dma, dma, dma, dma, dma, dma, dma,
             pltpu.SemaphoreType.REGULAR,
         ]
     )
     vmem, smem, hbm = (pl.BlockSpec(memory_space=s) for s in (pltpu.VMEM, pltpu.SMEM, pl.ANY))
-    received, row = pl.pallas_call(
+    received, edges, row = pl.pallas_call(
         functools.partial(kernel, n_rows, n_cols, blocks, tiles, pixel_total),
         out_shape=(
-            pltpu.VMEM((n_rows, blocks, HALF, TW), f32),
+            pieces,
+            pltpu.VMEM((2 * BR, blocks, 1, TW), f32),
             pltpu.VMEM((1, TW), f32),
         ),
         in_specs=[hbm, hbm, smem, vmem],
-        out_specs=(vmem, vmem),
+        out_specs=(vmem, vmem, vmem),
         scratch_shapes=scratch,
         compiler_params=pltpu.CompilerParams(collective_id=0, has_side_effects=True),
     )(
@@ -528,10 +642,10 @@
     out, objective = pl.pallas_call(
         assemble,
         out_shape=(jax.ShapeDtypeStruct((blocks, BR, width), f32), jax.ShapeDtypeStruct((ITERS,), f32)),
-        in_specs=[vmem, vmem],
+        in_specs=[vmem, vmem, vmem],
         out_specs=(hbm, smem),
         scratch_shapes=[pltpu.VMEM((blocks, BR, width), f32), dma((blocks,))],
-    )(pltpu.with_memory_space_constraint(received, pltpu.VMEM), pltpu.with_memory_space_constraint(row, pltpu.VMEM))
+    )(*(pltpu.with_memory_space_constraint(x, pltpu.VMEM) for x in (received, edges, row)))
     return out.reshape(rows_here, width), objective
 
 

time: 44.6 us -> 42 us (0.942)
  the two profiles are of different devices: /device:TPU:161 before, /device:TPU:1 now
where the time goes in v5:
time: 42 us; the launch traced here: 41.8 us
  Pallas kernels  41.2 us (98%)
  between operations  0.64 us (2%)
    pallas_call x1, Pallas kernels, per_device(): pl.pallas_call(functools.partial(kernel, n_rows, n_cols, blocks, tiles, p...  39.8 us
    pallas_call x1, Pallas kernels, per_device(): pl.pallas_call(assemble, out_shape=(jax.ShapeDtypeStruct((blocks, BR, wid...  1.39 us

profile of v5, /device:TPU:1, one launch (start us, length us, event | category | flops | bytes accessed | tf_op | source)
XLA Modules:
  0.0 41.8 jit_solution(7774688080488327219)
XLA Ops:
  0.6 39.8 %shard_map.59 = (f32[2,32,8,2,128]{4,3,2,1,0:T(2,128)S(1)}, f32[16,8,1,128]{3,2,1,0:T(1,128)S(1)}, f32[1,128]{1,0:T(1,128)S(1)}) custom-call(f32[8,8,2048]{2,1,0:T(8,128)} %bitcast.4, s32[8,8,2048]{2,1,0:T(8,128)} %bitcast.5, s32[8,16]{1,0:T(8,128)} %weight_ref.1, s32[1,256]{1,0:T(1,128)} %bitcast.6), custom_call_target="tpu_custom_call" | custom-call | tf_op jit(solution)/shard_map/pallas_call | solution.py:625
  40.4 1.4 %shard_map.60 = (f32[8,8,2048]{2,1,0:T(8,128)}, f32[3]{0:T(128)}) custom-call(f32[2,32,8,2,128]{4,3,2,1,0:T(2,128)S(1)} %get-tuple-element.7.pieces, f32[16,8,1,128]{3,2,1,0:T(1,128)S(1)} %get-tuple-element.8.edges, f32[1,128]{1,0:T(1,128)S(1)} %get-tuple-element.9.row), custom_call_target="tpu_custom_call" | custom-call | tf_op jit(solution)/shard_map/pallas_call | solution.py:642
